TPU v7x, 32 devices: a whole 2x2x4 slice. The times are simulated.
32 devices in a mesh: row: 4 (over y, core), col: 8 (over z, x).
Axes of the slice: x: 2, y: 2, z: 4, core: 2. Of those that a mesh axis runs over, the one named last changes fastest.
Arguments:
- sources: bfloat16 [4, 8, 4, 256, 256], P('row', 'col'), may hold values from -6 to 6
- history: bfloat16 [4, 8, 8, 256, 256], P(None, 'col'), may hold values from -4 to 4
- inverse_diagonal: float32 [4, 8, 256], P('row', 'col'), may hold values from 0.3 to 0.6
- far_cores: bfloat16 [4, 8, 32, 4, 8, 8, 32], P('row', None, None, None, 'col'), may hold values from -0.09375 to 0.09375
- target_basis: bfloat16 [4, 8, 256, 32], P('row', 'col'), may hold values from -1 to 1
- source_basis: bfloat16 [4, 8, 256, 32], P(None, 'col'), may hold values from -0.375 to 0.375
- near_blocks: bfloat16 [4, 8, 3, 256, 8, 256], P('row', 'col'), may hold values from -0.078125 to 0.078125
- near_tile: int32 [4, 8, 3], P('row', 'col'), may hold values from 0 to 3
- near_count: int32 [4, 8], P('row', 'col'), may hold values from 1 to 3, as said below
Outputs:
- new_steps: bfloat16 [4, 8, 4, 256, 256], P('row', 'col')
- energies: float32 [4, 256], replicated
Inputs may be any that keep to these rules, and one draw needn't show every extreme that they name: Only slots below near_count are used; in every draw some tile has all 3 slots live.
All inputs are finite; a program needn't handle non-finite values.
Results may differ from a plain program's by a relative error of at most 0.011.
Values may be sent and summed in bfloat16 or wider, within the bound.
A program may use at most 192 MiB of HBM per device.

v0:
```python
import functools

import jax
import jax.numpy as jnp
from jax import lax
from jax.experimental import pallas as pl
from jax.experimental.pallas import tpu as pltpu
from jax.sharding import PartitionSpec as P

MESH = pl.DeviceIdType.MESH
F32 = jnp.float32
BF16 = jnp.bfloat16


def march(
    rows,
    cols,
    panel_total,
    tiles_ref,
    count_ref,
    basis_hbm,
    history_hbm,
    cores_hbm,
    near_hbm,
    target_hbm,
    scaling_hbm,
    sources_hbm,
    steps_ref,
    energy_ref,
    basis,
    history,
    cores,
    near_blocks,
    target,
    scaling_row,
    sources,
    scaling,
    last_tile,
    cores_raw,
    near_raw,
    stage,
    past_proj,
    fresh_tiles,
    fresh_proj,
    core_out,
    core_in,
    near_sum,
    partial_sum,
    energy_own,
    energy_rows,
    energy_mid,
    energy_cols,
    load_sems,
    history_sems,
    result_sems,
    tile_send,
    tile_recv,
    pass_send,
    pass_recv,
    proj_send,
    proj_recv,
    core_send,
    core_recv,
    erow_send,
    erow_recv,
    ecol_send,
    ecol_recv,
):
    step_count = sources.shape[0]
    lag_count, _, rank, fields = past_proj.shape
    tile = history.shape[2]
    slot_count = near_blocks.shape[0]
    width = rows * rank
    my_row = lax.axis_index("row")
    my_col = lax.axis_index("col")
    partner = my_row + 1 - 2 * lax.rem(my_row, 2)

    def row_peer(d):
        return lax.rem(my_row + d, rows)

    def col_peer(d):
        return lax.rem(my_col + d, cols)

    loads = [
        pltpu.make_async_copy(src, dst, load_sems.at[n])
        for n, (src, dst) in enumerate(
            (
                (basis_hbm, basis),
                (cores_hbm, cores_raw),
                (near_hbm, near_raw),
                (target_hbm, target),
                (scaling_hbm, scaling_row),
                (sources_hbm, sources),
            )
        )
    ]

    def history_load(lag):
        return pltpu.make_async_copy(
            history_hbm.at[:, lag], history.at[:, lag], history_sems.at[lag]
        )

    loads[0].start()
    loads[1].start()
    for lag in range(lag_count):
        history_load(lag).start()
    for load in loads[2:]:
        load.start()

    barrier = pltpu.get_barrier_semaphore()
    for d in range(1, rows):
        pl.semaphore_signal(barrier, inc=1, device_id={"row": row_peer(d)}, device_id_type=MESH)
    for d in range(1, cols):
        pl.semaphore_signal(barrier, inc=1, device_id={"col": col_peer(d)}, device_id_type=MESH)

    def row_copy(src, dst, send, recv, to):
        return pltpu.make_async_remote_copy(
            src_ref=src, dst_ref=dst, send_sem=send, recv_sem=recv,
            device_id={"row": to}, device_id_type=MESH,
        )

    def col_copy(src, dst, send, recv, to):
        return pltpu.make_async_remote_copy(
            src_ref=src, dst_ref=dst, send_sem=send, recv_sem=recv,
            device_id={"col": to}, device_id_type=MESH,
        )

    def proj_copy(n, owner, d):
        return row_copy(
            fresh_proj.at[n, owner], fresh_proj.at[n, owner],
            proj_send.at[n, d], proj_recv.at[n, owner], row_peer(d),
        )

    def tile_copy(n, owner, d):
        return row_copy(
            fresh_tiles[n].at[owner], fresh_tiles[n].at[owner],
            tile_send.at[n, d], tile_recv.at[n, owner], row_peer(d),
        )

    def pass_copy(n, owner):
        return row_copy(
            fresh_tiles[n].at[owner], fresh_tiles[n].at[owner],
            pass_send.at[n, owner], pass_recv.at[n, owner], partner,
        )

    def core_copy(n, d):
        to = col_peer(d)
        return col_copy(
            core_out.at[n, to], core_in.at[n, my_col],
            core_send.at[n, d], core_recv.at[n, my_col], to,
        )

    def core_arrival(n, origin):
        return col_copy(
            core_out.at[n, origin], core_in.at[n, origin],
            core_send.at[n, 0], core_recv.at[n, origin], origin,
        )

    def result_copy(n):
        return pltpu.make_async_copy(
            fresh_tiles[n].at[my_row] if n + 1 < step_count else last_tile,
            steps_ref.at[n],
            result_sems.at[n],
        )

    def far_base(n):
        depth = lag_count - n
        total = jnp.dot(
            cores[:, n * width:],
            past_proj[0:depth].reshape(depth * width, fields),
            preferred_element_type=F32,
        )
        for lag in range(1, n):
            total += jnp.dot(
                cores[:, lag * width:(lag + 1) * width],
                fresh_proj[n - 1 - lag].reshape(width, fields),
                preferred_element_type=F32,
            )
        return total

    def near_base(n):
        depth = lag_count - n

        def add_slot(slot, carry):
            where = tiles_ref[slot]
            value = jnp.dot(
                near_blocks[slot, :, n * tile:],
                history[where, 0:depth].reshape(depth * tile, fields),
                preferred_element_type=F32,
            )
            for lag in range(1, n):
                value += jnp.dot(
                    near_blocks[slot, :, lag * tile:(lag + 1) * tile],
                    fresh_tiles[n - 1 - lag][where],
                    preferred_element_type=F32,
                )
            near_sum[n] += value
            return carry

        near_sum[n] = jnp.zeros((tile, fields), F32)
        lax.fori_loop(0, slot_count, add_slot, 0)

    def near_fresh(n):
        total = near_sum[n]
        for slot in range(slot_count):
            total += jnp.dot(
                near_blocks[slot, :, 0:tile],
                fresh_tiles[n - 1][tiles_ref[slot]],
                preferred_element_type=F32,
            )
        near_sum[n] = sources[n].astype(F32) - total

    lanes = stage.shape[2]
    block = stage.shape[1] // lag_count

    def spread(value):
        for c in range(value.shape[1] // lanes):
            stage[c] = value[:, c * lanes:(c + 1) * lanes]

    def pick(lag, c):
        return stage[c, pl.ds(lag, block, stride=lag_count), :].astype(BF16)

    def pack_cores(g, carry):
        here = pl.ds(pl.multiple_of(g * block, block), block)
        total = None
        for p in range(rows):
            value = cores_raw[here, p].astype(F32).reshape(block * lag_count, rank).astype(BF16)
            place = (
                lax.broadcasted_iota(jnp.int32, (rank, width), 1)
                == lax.broadcasted_iota(jnp.int32, (rank, width), 0) + p * rank
            )
            term = jnp.dot(
                value, place.astype(F32).astype(BF16), preferred_element_type=F32
            )
            total = term if total is None else total + term
        spread(total)
        for lag in range(lag_count):
            for c in range(width // lanes):
                first = lag * width + c * lanes
                cores[here, first:first + lanes] = pick(lag, c)
        return carry

    def pack_near(index, carry):
        slot = index // (tile // block)
        here = pl.ds(pl.multiple_of(lax.rem(index, tile // block) * block, block), block)
        spread(near_raw[slot, here].astype(F32).reshape(block * lag_count, tile))
        for lag in range(lag_count):
            for c in range(tile // lanes):
                first = lag * tile + c * lanes
                near_blocks[slot, here, first:first + lanes] = jnp.where(
                    slot < count_ref[0], pick(lag, c), jnp.zeros((block, lanes), BF16)
                )
        return carry

    loads[1].wait()
    lax.fori_loop(0, cores.shape[0] // block, pack_cores, 0)
    loads[0].wait()

    def project_lag(lag, carry):
        history_load(lag).wait()
        for p in range(rows):
            past_proj[lag, p] = jnp.dot(
                basis[p], history[p, lag], preferred_element_type=F32
            ).astype(BF16)
        return carry

    lax.fori_loop(0, lag_count, project_lag, 0)

    for n in range(step_count):
        if n == 0:
            partial = far_base(0)
        else:
            for d in range(1, rows):
                proj_copy(n - 1, row_peer(d), d).wait_recv()
            partial = partial_sum[...] + jnp.dot(
                cores[:, 0:width],
                fresh_proj[n - 1].reshape(width, fields),
                preferred_element_type=F32,
            )
        core_out[n] = partial.astype(BF16).reshape(cols, rank, fields)
        if n == 0:
            pl.semaphore_wait(barrier, rows - 1 + cols - 1)
        for d in range(1, cols):
            core_copy(n, d).start()
        if n == 0:
            loads[2].wait()
            lax.fori_loop(0, slot_count * (tile // block), pack_near, 0)
            near_base(0)
            for load in loads[3:]:
                load.wait()
            scaling[...] = jnp.transpose(jnp.broadcast_to(scaling_row[...], (fields, tile)))
            near_sum[0] = sources[0].astype(F32) - near_sum[0]
        else:
            near_base(n)
            for d in range(2, rows, 2):
                tile_copy(n - 1, row_peer(d), d).wait_recv()
                pass_copy(n - 1, row_peer(d)).start()
            tile_copy(n - 1, partner, 1).wait_recv()
            for d in range(2, rows, 2):
                pass_copy(n - 1, lax.rem(partner + d, rows)).wait_recv()
            near_fresh(n)
        core = core_out[n, my_col].astype(F32)
        for d in range(1, cols):
            origin = col_peer(d)
            core_arrival(n, origin).wait_recv()
            core += core_in[n, origin].astype(F32)
        far = lax.dot_general(
            target[...], core.astype(BF16), (((0,), (0,)), ((), ())),
            preferred_element_type=F32,
        )
        fresh = (scaling[...] * (near_sum[n] - far)).astype(BF16)
        if n + 1 < step_count:
            fresh_tiles[n][my_row] = fresh
            row_copy(
                fresh_tiles[n].at[my_row], fresh_tiles[n].at[my_row],
                tile_send.at[n, 0], tile_recv.at[n, my_row], partner,
            ).start()
            fresh_proj[n, my_row] = jnp.dot(
                basis[my_row], fresh, preferred_element_type=F32
            ).astype(BF16)
            for d in range(1, rows):
                proj_copy(n, my_row, d).start()
            for d in range(2, rows, 2):
                tile_copy(n, my_row, d).start()
        else:
            last_tile[...] = fresh
        result_copy(n).start()
        energy_own[n:n + 1, :] = (
            jnp.sum(jnp.square(fresh.astype(F32)), axis=0, keepdims=True) / panel_total
        )
        if n + 1 < step_count:
            partial_sum[...] = far_base(n + 1)

    def erow_copy(origin, d):
        return row_copy(
            energy_own, energy_rows.at[origin], erow_send.at[d], erow_recv.at[origin], row_peer(d)
        )

    def ecol_copy(origin, d):
        return col_copy(
            energy_mid, energy_cols.at[origin], ecol_send.at[d], ecol_recv.at[origin], col_peer(d)
        )

    for d in range(1, rows):
        erow_copy(my_row, d).start()
    energy_rows[my_row] = energy_own[...]
    for d in range(1, rows):
        erow_copy(row_peer(d), d).wait_recv()
    total = energy_rows[0]
    for p in range(1, rows):
        total += energy_rows[p]
    energy_mid[...] = total
    for d in range(1, cols):
        ecol_copy(my_col, d).start()
    energy_cols[my_col] = total
    for d in range(1, cols):
        ecol_copy(col_peer(d), d).wait_recv()
    total = energy_cols[0]
    for q in range(1, cols):
        total += energy_cols[q]
    energy_ref[...] = total

    for n in range(step_count):
        result_copy(n).wait()
        for d in range(1, cols):
            core_copy(n, d).wait_send()
        if n + 1 < step_count:
            row_copy(
                fresh_tiles[n].at[my_row], fresh_tiles[n].at[my_row],
                tile_send.at[n, 0], tile_recv.at[n, my_row], partner,
            ).wait_send()
            for d in range(1, rows):
                proj_copy(n, my_row, d).wait_send()
            for d in range(2, rows, 2):
                tile_copy(n, my_row, d).wait_send()
                pass_copy(n, row_peer(d)).wait_send()
    for d in range(1, rows):
        erow_copy(my_row, d).wait_send()
    for d in range(1, cols):
        ecol_copy(my_col, d).wait_send()


def hand_over(steps_in, energy_in, steps_out, energy_out):
    steps_out[...] = steps_in[...]
    energy_out[...] = energy_in[...]


def local(
    sources,
    history,
    inverse_diagonal,
    far_cores,
    target_basis,
    source_basis,
    near_blocks,
    near_tile,
    near_count,
):
    rows, _, lags, tile, fields = history.shape
    cols, rank = far_cores.shape[1:3]
    steps = sources.shape[2]
    slots = near_blocks.shape[2]
    panel_total = rows * cols * tile
    lanes = min(128, tile, rows * rank)
    block = min(64, tile)
    dma = pltpu.SemaphoreType.DMA
    anywhere = pl.BlockSpec(memory_space=pltpu.HBM)
    scalar = pl.BlockSpec(memory_space=pltpu.SMEM)
    inside = pl.BlockSpec(memory_space=pltpu.VMEM)
    new_steps, energies = pl.pallas_call(
        functools.partial(march, rows, cols, panel_total),
        out_shape=(
            jax.ShapeDtypeStruct((steps, tile, fields), BF16),
            jax.ShapeDtypeStruct((steps, fields), F32),
        ),
        in_specs=[scalar, scalar] + [anywhere] * 7,
        out_specs=(anywhere, inside),
        scratch_shapes=[
            pltpu.VMEM((rows, rank, tile), BF16),
            pltpu.VMEM((rows, lags, tile, fields), BF16),
            pltpu.VMEM((cols * rank, lags * rows * rank), BF16),
            pltpu.VMEM((slots, tile, lags * tile), BF16),
            pltpu.VMEM((rank, tile), BF16),
            pltpu.VMEM((1, tile), F32),
            pltpu.VMEM((steps, tile, fields), BF16),
            pltpu.VMEM((tile, fields), F32),
            pltpu.VMEM((tile, fields), BF16),
            pltpu.VMEM((cols * rank, rows, lags, rank), BF16),
            pltpu.VMEM((slots, tile, lags, tile), BF16),
            pltpu.VMEM((max(tile, rows * rank) // lanes, block * lags, lanes), F32),
            pltpu.VMEM((lags, rows, rank, fields), BF16),
            tuple(pltpu.VMEM((rows, tile, fields), BF16) for _ in range(steps - 1)),
            pltpu.VMEM((steps - 1, rows, rank, fields), BF16),
            pltpu.VMEM((steps, cols, rank, fields), BF16),
            pltpu.VMEM((steps, cols, rank, fields), BF16),
            pltpu.VMEM((steps, tile, fields), F32),
            pltpu.VMEM((cols * rank, fields), F32),
            pltpu.VMEM((steps, fields), F32),
            pltpu.VMEM((rows, steps, fields), F32),
            pltpu.VMEM((steps, fields), F32),
            pltpu.VMEM((cols, steps, fields), F32),
            dma((6,)),
            dma((lags,)),
            dma((steps,)),
            dma((steps - 1, rows)),
            dma((steps - 1, rows)),
            dma((steps - 1, rows)),
            dma((steps - 1, rows)),
            dma((steps - 1, rows)),
            dma((steps - 1, rows)),
            dma((steps, cols)),
            dma((steps, cols)),
            dma((rows,)),
            dma((rows,)),
            dma((cols,)),
            dma((cols,)),
        ],
        compiler_params=pltpu.CompilerParams(
            collective_id=0, has_side_effects=True, vmem_limit_bytes=58 * 1024 * 1024
        ),
    )(
        near_tile.reshape(slots),
        near_count.reshape(1),
        jnp.swapaxes(source_basis[:, 0], 1, 2),
        history[:, 0],
        far_cores.reshape(cols * rank, rows, lags, rank),
        near_blocks[0, 0],
        jnp.swapaxes(target_basis[0, 0], 0, 1),
        inverse_diagonal[0],
        sources[0, 0],
    )
    new_steps, energies = pl.pallas_call(
        hand_over,
        out_shape=(
            jax.ShapeDtypeStruct((steps, tile, fields), BF16),
            jax.ShapeDtypeStruct((steps, fields), F32),
        ),
        in_specs=(inside, inside),
        out_specs=(inside, inside),
    )(new_steps, energies)
    return new_steps[None, None], energies


def solution(mesh):
    placed = (
        P("row", "col", None, None, None),
        P(None, "col", None, None, None),
        P("row", "col", None),
        P("row", None, None, None, "col", None, None),
        P("row", "col", None, None),
        P(None, "col", None, None),
        P("row", "col", None, None, None, None),
        P("row", "col", None),
        P("row", "col"),
    )
    return jax.shard_map(
        local,
        mesh=mesh,
        in_specs=placed,
        out_specs=(P("row", "col", None, None, None), P()),
        check_vma=False,
    )
```

profile of v0, /device:TPU:0, one launch (start us, length us, event | category | flops | bytes accessed | tf_op | source)
XLA Modules:
  0.0 51.9 jit_solution(14783068041252925864)
XLA Ops:
  1.3 48.7 %shard_map.104 = (bf16[4,256,256]{2,1,0:T(8,128)(2,1)}, f32[4,256]{1,0:T(4,128)}) custom-call(s32[3]{0:T(128)} %bitcast.22, s32[1]{0:T(128)} %bitcast.14.count_ref, bf16[4,32,256]{2,1,0:T(8,128)(2,1)} %bitcast.19, bf16[4,8,256,256]{3,2,1,0:T(8,128)(2,1)} %bitcast.15, bf16[256,4,8,32]{3,2,1,0:T(8,128)(2,1)} %bitcast.17, bf16[3,256,8,256]{3,2,1,0:T(8,128)(2,1)} %bitcast.16, ...), custom_call_target="tpu_custom_call" | custom-call | tf_op jit(solution)/shard_map/pallas_call | solution.py:410
  50.0 1.9 %shard_map.105 = (bf16[4,256,256]{2,1,0:T(8,128)(2,1)}, f32[4,256]{1,0:T(4,128)}) custom-call(bf16[4,256,256]{2,1,0:T(8,128)(2,1)} %get-tuple-element.6.steps_in, f32[4,256]{1,0:T(4,128)} %get-tuple-element.7.energy_in), custom_call_target="tpu_custom_call" | custom-call | tf_op jit(solution)/shard_map/pallas_call | solution.py:472
where the time goes:
time: 52.1 us; the launch traced here: 51.9 us
  Pallas kernels  50.6 us (97%)
  between operations  1.29 us (2%)
    pallas_call x1, Pallas kernels, local(): pl.pallas_call(functools.partial(march, rows, cols, panel_total), out_sha...  48.7 us
    pallas_call x1, Pallas kernels, local(): pl.pallas_call(hand_over, out_shape=(jax.ShapeDtypeStruct((steps, tile, f...  1.87 us

commit v1 on v0

v1 whole, which is shorter than its diff:
```python
import functools

import jax
import jax.numpy as jnp
from jax import lax
from jax.experimental import pallas as pl
from jax.experimental.pallas import tpu as pltpu
from jax.sharding import PartitionSpec as P

MESH = pl.DeviceIdType.MESH
F32 = jnp.float32
BF16 = jnp.bfloat16


def march(
    rows,
    cols,
    panel_total,
    tiles_hbm,
    count_hbm,
    basis_hbm,
    history_hbm,
    cores_hbm,
    near_hbm,
    target_hbm,
    scaling_hbm,
    sources_hbm,
    steps_ref,
    energy_ref,
    tiles_ref,
    count_ref,
    basis,
    history,
    cores,
    near_blocks,
    target,
    scaling_row,
    sources,
    scaling,
    cores_raw,
    near_raw,
    stage,
    past_proj,
    fresh_tiles,
    fresh_proj,
    core_out,
    core_in,
    near_sum,
    partial_sum,
    energy_own,
    energy_early,
    energy_last,
    load_sems,
    history_sems,
    tile_send,
    tile_recv,
    pass_send,
    pass_recv,
    proj_send,
    proj_recv,
    core_send,
    core_recv,
    energy_send,
    energy_recv,
):
    step_count = sources.shape[0]
    lag_count, _, rank, fields = past_proj.shape
    tile = history.shape[2]
    slot_count = near_blocks.shape[0]
    width = rows * rank
    my_row = lax.axis_index("row")
    my_col = lax.axis_index("col")
    partner = my_row + 1 - 2 * lax.rem(my_row, 2)

    def row_peer(d):
        return lax.rem(my_row + d, rows)

    def col_peer(d):
        return lax.rem(my_col + d, cols)

    loads = [
        pltpu.make_async_copy(src, dst, load_sems.at[n])
        for n, (src, dst) in enumerate(
            (
                (basis_hbm, basis),
                (cores_hbm, cores_raw),
                (near_hbm, near_raw),
                (target_hbm, target),
                (scaling_hbm, scaling_row),
                (sources_hbm, sources),
                (tiles_hbm, tiles_ref),
                (count_hbm, count_ref),
            )
        )
    ]

    pairs = [(lag, min(2, lag_count - lag)) for lag in range(0, lag_count, 2)]

    def history_load(index):
        first, length = pairs[index]
        return pltpu.make_async_copy(
            history_hbm.at[:, first:first + length],
            history.at[:, first:first + length],
            history_sems.at[index],
        )

    def wait_bytes(ref, sem):
        pltpu.make_async_copy(ref, ref, sem).wait()

    loads[1].start()
    loads[0].start()
    for index in range(len(pairs)):
        history_load(index).start()

    barrier = pltpu.get_barrier_semaphore()
    peers = [(a, b) for a in range(rows) for b in range(cols) if a or b]

    def greet(index, carry):
        pl.semaphore_signal(
            barrier, inc=1, device_id=(row_peer(index // cols), col_peer(lax.rem(index, cols))),
            device_id_type=MESH,
        )
        return carry

    lax.fori_loop(1, rows * cols, greet, 0)

    def row_copy(src, dst, send, recv, to):
        return pltpu.make_async_remote_copy(
            src_ref=src, dst_ref=dst, send_sem=send, recv_sem=recv,
            device_id={"row": to}, device_id_type=MESH,
        )

    def col_copy(src, dst, send, recv, to):
        return pltpu.make_async_remote_copy(
            src_ref=src, dst_ref=dst, send_sem=send, recv_sem=recv,
            device_id={"col": to}, device_id_type=MESH,
        )

    def proj_copy(n, owner, d):
        return row_copy(
            fresh_proj.at[n, owner], fresh_proj.at[n, owner],
            proj_send.at[n], proj_recv.at[n], row_peer(d),
        )

    def tile_copy(n, owner, d):
        return row_copy(
            fresh_tiles[n].at[owner], fresh_tiles[n].at[owner],
            tile_send.at[n], tile_recv.at[n, owner // 2], row_peer(d),
        )

    def pass_copy(n, owner):
        return row_copy(
            fresh_tiles[n].at[owner], fresh_tiles[n].at[owner],
            pass_send.at[n], pass_recv.at[n], partner,
        )

    def core_copy(n, d):
        to = col_peer(d)
        return col_copy(
            core_out.at[n, to], core_in.at[n, my_col],
            core_send.at[n], core_recv.at[n], to,
        )

    me = my_row * cols + my_col

    def energy_copy(last, owner, d):
        return pltpu.make_async_remote_copy(
            src_ref=energy_own.at[step_count - 1] if last else energy_own.at[0:step_count - 1],
            dst_ref=energy_last.at[owner] if last else energy_early.at[owner],
            send_sem=energy_send.at[last],
            recv_sem=energy_recv.at[last],
            device_id=(row_peer(peers[d][0]), col_peer(peers[d][1])),
            device_id_type=MESH,
        )

    def far_base(n):
        depth = lag_count - n
        total = jnp.dot(
            cores[:, n * width:],
            past_proj[0:depth].reshape(depth * width, fields),
            preferred_element_type=F32,
        )
        for lag in range(1, n):
            total += jnp.dot(
                cores[:, lag * width:(lag + 1) * width],
                fresh_proj[n - 1 - lag].reshape(width, fields),
                preferred_element_type=F32,
            )
        return total

    def near_base(n):
        depth = lag_count - n

        def add_slot(slot, carry):
            where = tiles_ref[0, 0, slot]
            value = jnp.dot(
                near_blocks[slot, :, n * tile:],
                history[where, 0:depth].reshape(depth * tile, fields),
                preferred_element_type=F32,
            )
            for lag in range(1, n):
                value += jnp.dot(
                    near_blocks[slot, :, lag * tile:(lag + 1) * tile],
                    fresh_tiles[n - 1 - lag][where],
                    preferred_element_type=F32,
                )
            near_sum[n] += value
            return carry

        near_sum[n] = jnp.zeros((tile, fields), F32)
        lax.fori_loop(0, slot_count, add_slot, 0)

    def near_fresh(n):
        total = near_sum[n]
        for slot in range(slot_count):
            total += jnp.dot(
                near_blocks[slot, :, 0:tile],
                fresh_tiles[n - 1][tiles_ref[0, 0, slot]],
                preferred_element_type=F32,
            )
        near_sum[n] = sources[n].astype(F32) - total

    lanes = stage.shape[2]
    block = stage.shape[1] // lag_count

    def spread(value, base=0):
        for c in range(value.shape[1] // lanes):
            stage[base + c] = value[:, c * lanes:(c + 1) * lanes]

    def pick(lag, c):
        return stage[c, pl.ds(lag, block, stride=lag_count), :].astype(BF16)

    def pack_cores(g):
        here = pl.ds(g * block, block)
        base = g % 2 * (width // lanes)
        total = None
        for p in range(rows):
            value = cores_raw[here, p].astype(F32).reshape(block * lag_count, rank).astype(BF16)
            place = (
                lax.broadcasted_iota(jnp.int32, (rank, width), 1)
                == lax.broadcasted_iota(jnp.int32, (rank, width), 0) + p * rank
            )
            term = jnp.dot(
                value, place.astype(F32).astype(BF16), preferred_element_type=F32
            )
            total = term if total is None else total + term
        spread(total, base)
        for lag in range(lag_count):
            for c in range(width // lanes):
                first = lag * width + c * lanes
                cores[here, first:first + lanes] = pick(lag, base + c)

    def pack_near(index, carry):
        slot = index // (tile // block)
        here = pl.ds(pl.multiple_of(lax.rem(index, tile // block) * block, block), block)
        spread(near_raw[slot, here].astype(F32).reshape(block * lag_count, tile))
        for lag in range(lag_count):
            for c in range(tile // lanes):
                first = lag * tile + c * lanes
                near_blocks[slot, here, first:first + lanes] = jnp.where(
                    slot < count_ref[0, 0], pick(lag, c), jnp.zeros((block, lanes), BF16)
                )
        return carry

    loads[1].wait()
    for load in loads[2:]:
        load.start()
    for g in range(cores.shape[0] // block):
        pack_cores(g)
    loads[0].wait()
    for index, (first, length) in enumerate(pairs):
        history_load(index).wait()
        for lag in range(first, first + length):
            for p in range(rows):
                past_proj[lag, p] = jnp.dot(
                    basis[p], history[p, lag], preferred_element_type=F32
                ).astype(BF16)

    far_first = sorted(range(1, cols), key=lambda d: -min(d, cols - d))
    for n in range(step_count):
        if n == 0:
            partial = far_base(0)
        else:
            wait_bytes(fresh_proj.at[n - 1, 0:rows - 1], proj_recv.at[n - 1])
            partial = partial_sum[...] + jnp.dot(
                cores[:, 0:width],
                fresh_proj[n - 1].reshape(width, fields),
                preferred_element_type=F32,
            )
        core_out[n] = partial.astype(BF16).reshape(cols, rank, fields)
        if n == 0:
            pl.semaphore_wait(barrier, rows * cols - 1)
        for d in far_first:
            core_copy(n, d).start()
        if n + 1 == step_count:
            for d in range(len(peers)):
                energy_copy(0, me, d).start()
        if n == 0:
            for load in (loads[2], *loads[6:]):
                load.wait()
            lax.fori_loop(0, slot_count * (tile // block), pack_near, 0)
            near_base(0)
            for load in loads[3:6]:
                load.wait()
            scaling[...] = jnp.transpose(jnp.broadcast_to(scaling_row[...], (fields, tile)))
            near_sum[0] = sources[0].astype(F32) - near_sum[0]
        else:
            near_base(n)
            for d in range(2, rows, 2):
                tile_copy(n - 1, row_peer(d), d).wait_recv()
                pass_copy(n - 1, row_peer(d)).start()
            tile_copy(n - 1, partner, 1).wait_recv()
            wait_bytes(fresh_tiles[n - 1].at[0:rows // 2 - 1], pass_recv.at[n - 1])
            near_fresh(n)
        core = core_out[n, my_col].astype(F32)
        wait_bytes(core_in.at[n, 0:cols - 1], core_recv.at[n])
        for d in range(1, cols):
            core += core_in[n, col_peer(d)].astype(F32)
        far = lax.dot_general(
            target[...], core.astype(BF16), (((0,), (0,)), ((), ())),
            preferred_element_type=F32,
        )
        fresh = (scaling[...] * (near_sum[n] - far)).astype(BF16)
        if n + 1 < step_count:
            fresh_tiles[n][my_row] = fresh
            row_copy(
                fresh_tiles[n].at[my_row], fresh_tiles[n].at[my_row],
                tile_send.at[n], tile_recv.at[n, my_row // 2], partner,
            ).start()
            fresh_proj[n, my_row] = jnp.dot(
                basis[my_row], fresh, preferred_element_type=F32
            ).astype(BF16)
            for d in range(1, rows):
                proj_copy(n, my_row, d).start()
            for d in range(2, rows, 2):
                tile_copy(n, my_row, d).start()
            steps_ref[n] = fresh
        else:
            steps_ref[n] = fresh
        energy_own[n] = (
            jnp.sum(jnp.square(fresh.astype(F32)), axis=0, keepdims=True) / panel_total
        )
        if n + 1 < step_count:
            partial_sum[...] = far_base(n + 1)

    for d in range(len(peers)):
        energy_copy(1, me, d).start()
    energy_early[me] = energy_own[0:step_count - 1]
    energy_last[me] = energy_own[step_count - 1]
    for last, where in ((0, energy_early), (1, energy_last)):
        wait_bytes(where.at[0:len(peers)], energy_recv.at[last])
        total = where[0]
        for origin in range(1, rows * cols):
            total += where[origin]
        if last:
            energy_ref[step_count - 1:step_count, :] = total
        else:
            for n in range(step_count - 1):
                energy_ref[n:n + 1, :] = total[n]

    for n in range(step_count):
        wait_bytes(core_in.at[n, 0:cols - 1], core_send.at[n])
        if n + 1 < step_count:
            wait_bytes(fresh_proj.at[n, 0:rows - 1], proj_send.at[n])
            wait_bytes(fresh_tiles[n].at[0:rows // 2], tile_send.at[n])
            wait_bytes(fresh_tiles[n].at[0:rows // 2 - 1], pass_send.at[n])
    wait_bytes(energy_early.at[0:len(peers)], energy_send.at[0])
    wait_bytes(energy_last.at[0:len(peers)], energy_send.at[1])


def hand_over(steps_in, energy_in, steps_out, energy_out, sems):
    copies = (
        pltpu.make_async_copy(steps_in, steps_out, sems.at[0]),
        pltpu.make_async_copy(energy_in, energy_out, sems.at[1]),
    )
    for copy in copies:
        copy.start()
    for copy in copies:
        copy.wait()


def local(
    sources,
    history,
    inverse_diagonal,
    far_cores,
    target_basis,
    source_basis,
    near_blocks,
    near_tile,
    near_count,
):
    rows, _, lags, tile, fields = history.shape
    cols, rank = far_cores.shape[1:3]
    steps = sources.shape[2]
    slots = near_blocks.shape[2]
    panel_total = rows * cols * tile
    lanes = min(128, tile, rows * rank)
    block = min(64, tile)
    dma = pltpu.SemaphoreType.DMA
    anywhere = pl.BlockSpec(memory_space=pltpu.HBM)
    inside = pl.BlockSpec(memory_space=pltpu.VMEM)
    new_steps, energies = pl.pallas_call(
        functools.partial(march, rows, cols, panel_total),
        out_shape=(
            pltpu.VMEM((steps, tile, fields), BF16),
            pltpu.VMEM((steps, fields), F32),
        ),
        in_specs=[anywhere] * 9,
        out_specs=(inside, inside),
        scratch_shapes=[
            pltpu.SMEM((1, 1, slots), jnp.int32),
            pltpu.SMEM((1, 1), jnp.int32),
            pltpu.VMEM((rows, rank, tile), BF16),
            pltpu.VMEM((rows, lags, tile, fields), BF16),
            pltpu.VMEM((cols * rank, lags * rows * rank), BF16),
            pltpu.VMEM((slots, tile, lags * tile), BF16),
            pltpu.VMEM((rank, tile), BF16),
            pltpu.VMEM((1, tile), F32),
            pltpu.VMEM((steps, tile, fields), BF16),
            pltpu.VMEM((tile, fields), F32),
            pltpu.VMEM((cols * rank, rows, lags, rank), BF16),
            pltpu.VMEM((slots, tile, lags, tile), BF16),
            pltpu.VMEM((max(tile, 2 * rows * rank) // lanes, block * lags, lanes), F32),
            pltpu.VMEM((lags, rows, rank, fields), BF16),
            tuple(pltpu.VMEM((rows, tile, fields), BF16) for _ in range(steps - 1)),
            pltpu.VMEM((steps - 1, rows, rank, fields), BF16),
            pltpu.VMEM((steps, cols, rank, fields), BF16),
            pltpu.VMEM((steps, cols, rank, fields), BF16),
            pltpu.VMEM((steps, tile, fields), F32),
            pltpu.VMEM((cols * rank, fields), F32),
            pltpu.VMEM((steps, 1, fields), F32),
            pltpu.VMEM((rows * cols, steps - 1, 1, fields), F32),
            pltpu.VMEM((rows * cols, 1, fields), F32),
            dma((8,)),
            dma(((lags + 1) // 2,)),
            dma((steps - 1,)),
            dma((steps - 1, rows // 2)),
            dma((steps - 1,)),
            dma((steps - 1,)),
            dma((steps - 1,)),
            dma((steps - 1,)),
            dma((steps,)),
            dma((steps,)),
            dma((2,)),
            dma((2,)),
        ],
        compiler_params=pltpu.CompilerParams(
            collective_id=0, has_side_effects=True, vmem_limit_bytes=58 * 1024 * 1024
        ),
    )(
        near_tile,
        near_count,
        jnp.swapaxes(source_basis[:, 0], 1, 2),
        history[:, 0],
        far_cores.reshape(cols * rank, rows, lags, rank),
        near_blocks[0, 0],
        jnp.swapaxes(target_basis[0, 0], 0, 1),
        inverse_diagonal[0],
        sources[0, 0],
    )
    new_steps, energies = pl.pallas_call(
        hand_over,
        out_shape=(
            jax.ShapeDtypeStruct((steps, tile, fields), BF16),
            jax.ShapeDtypeStruct((steps, fields), F32),
        ),
        in_specs=(inside, inside),
        out_specs=(anywhere, anywhere),
        scratch_shapes=[dma((2,))],
    )(
        pltpu.with_memory_space_constraint(new_steps, pltpu.VMEM),
        pltpu.with_memory_space_constraint(energies, pltpu.VMEM),
    )
    return new_steps[None, None], energies


def solution(mesh):
    placed = (
        P("row", "col", None, None, None),
        P(None, "col", None, None, None),
        P("row", "col", None),
        P("row", None, None, None, "col", None, None),
        P("row", "col", None, None),
        P(None, "col", None, None),
        P("row", "col", None, None, None, None),
        P("row", "col", None),
        P("row", "col"),
    )
    return jax.shard_map(
        local,
        mesh=mesh,
        in_specs=placed,
        out_specs=(P("row", "col", None, None, None), P()),
        check_vma=False,
    )
```

time: 52.1 us -> 47.9 us (0.919)
  Pallas kernels: 50.6 us -> 46.5 us
    pallas_call x1, Pallas kernels: 48.7 us -> 45.7 us  [local(): pl.pallas_call(functools.partial(march, rows, cols, panel_total), out_sha...]
    pallas_call x1, Pallas kernels: 1.87 us -> 0.81 us  [local(): pl.pallas_call(hand_over, out_shape=(jax.ShapeDtypeStruct((steps, tile, f...]
where the time goes in v1:
time: 47.9 us; the launch traced here: 47.8 us
  Pallas kernels  46.5 us (97%)
  between operations  1.29 us (3%)
    pallas_call x1, Pallas kernels, local(): pl.pallas_call(functools.partial(march, rows, cols, panel_total), out_sha...  45.7 us

profile of v1, /device:TPU:0, one launch (start us, length us, event | category | flops | bytes accessed | tf_op | source)
XLA Modules:
  0.0 47.8 jit_solution(18271985398343486287)
XLA Ops:
  1.3 45.7 %shard_map.104 = (bf16[4,256,256]{2,1,0:T(8,128)(2,1)S(1)}, f32[4,256]{1,0:T(4,128)S(1)}) custom-call(s32[1,1,3]{2,1,0:T(1,128)} %tiles_hbm.1, s32[1,1]{1,0:T(1,128)S(6)} %copy.11.count_hbm, bf16[4,32,256]{2,1,0:T(8,128)(2,1)} %bitcast.16, bf16[4,8,256,256]{3,2,1,0:T(8,128)(2,1)} %bitcast.12, bf16[256,4,8,32]{3,2,1,0:T(8,128)(2,1)} %bitcast.14, ...), custom_call_target="tpu_custom_call" | custom-call | tf_op jit(solution)/shard_map/pallas_call | solution.py:403
  47.0 0.8 %shard_map.105 = (bf16[4,256,256]{2,1,0:T(8,128)(2,1)}, f32[4,256]{1,0:T(4,128)}) custom-call(bf16[4,256,256]{2,1,0:T(8,128)(2,1)S(1)} %get-tuple-element.6.steps_in, f32[4,256]{1,0:T(4,128)S(1)} %get-tuple-element.7.energy_in), custom_call_target="tpu_custom_call" | custom-call | tf_op jit(solution)/shard_map/pallas_call | solution.py:462

commit v2 on v1

v2 whole, which is shorter than its diff:
```python
import contextlib
import functools

import jax
import jax.numpy as jnp
from jax import lax
from jax.experimental import pallas as pl
from jax.experimental.pallas import tpu as pltpu
from jax.sharding import PartitionSpec as P

MESH = pl.DeviceIdType.MESH
F32 = jnp.float32
BF16 = jnp.bfloat16
scope = contextlib.nullcontext


def march(
    rows,
    cols,
    panel_total,
    tiles_hbm,
    count_hbm,
    basis_hbm,
    history_hbm,
    cores_hbm,
    near_hbm,
    target_hbm,
    scaling_hbm,
    sources_hbm,
    steps_ref,
    energy_ref,
    tiles_ref,
    count_ref,
    basis,
    history,
    cores,
    near_blocks,
    target,
    scaling_row,
    sources,
    scaling,
    cores_raw,
    near_raw,
    stage,
    past_proj,
    lifts,
    mixer,
    hub_cores,
    lead,
    older_out,
    older_in,
    first_out,
    first_in,
    sums_out,
    sums_in,
    sums_base,
    pairs,
    drive,
    plane_proj,
    drive_tiles,
    fresh_tiles,
    near_sum,
    energy_own,
    energy_early,
    energy_last,
    load_sems,
    history_sems,
    start_send,
    start_recv,
    older_send,
    older_recv,
    drive_send,
    drive_recv,
    plane_send,
    plane_recv,
    pair_send,
    pair_recv,
    sums_send,
    sums_recv,
    tile_send,
    tile_recv,
    pass_send,
    pass_recv,
    energy_send,
    energy_recv,
):
    step_count = sources.shape[0]
    lag_count, _, rank, fields = past_proj.shape
    tile = history.shape[2]
    slot_count = near_blocks.shape[0]
    width = rows * rank
    chips = rows // 2
    depths = cols // 2
    my_row = lax.axis_index("row")
    my_col = lax.axis_index("col")
    side = lax.rem(my_row, 2)
    chip = my_row // 2
    my_z = my_col // 2
    my_x = lax.rem(my_col, 2)
    partner = my_row + 1 - 2 * side
    hub_row = 2 * chip + 1
    is_hub = side == 1
    own_pair = pl.ds(2 * chip, 2)
    plane_pair = pl.ds(my_x * rows + 2 * chip, 2)
    me = my_row * cols + my_col

    def row_peer(d):
        return lax.rem(my_row + d, rows)

    def col_peer(d):
        return lax.rem(my_col + d, cols)

    def far_depth(i):
        up = i + (i - my_z + depths) // depths
        mirrored = depths - 1 - my_z
        down = depths - 1 - (i + (i - mirrored + depths) // depths)
        upper = 2 * my_z // depths
        return upper * up + (1 - upper) * down

    loads = [
        pltpu.make_async_copy(src, dst, load_sems.at[n])
        for n, (src, dst) in enumerate(
            (
                (basis_hbm, basis),
                (cores_hbm, cores_raw),
                (near_hbm, near_raw),
                (target_hbm, target),
                (scaling_hbm, scaling_row),
                (sources_hbm, sources),
                (tiles_hbm, tiles_ref),
                (count_hbm, count_ref),
            )
        )
    ]
    spans = [(lag, min(2, lag_count - lag)) for lag in range(0, lag_count, 2)]

    def history_load(index):
        first, length = spans[index]
        return pltpu.make_async_copy(
            history_hbm.at[:, first:first + length],
            history.at[:, first:first + length],
            history_sems.at[index],
        )

    def wait_bytes(ref, sem):
        pltpu.make_async_copy(ref, ref, sem).wait()

    for load in (loads[1], loads[0], *loads[3:5]):
        load.start()
    for index in range(len(spans)):
        history_load(index).start()

    barrier = pltpu.get_barrier_semaphore()
    peers = [(a, b) for a in range(rows) for b in range(cols) if a or b]

    def greet(index, carry):
        pl.semaphore_signal(
            barrier, inc=1, device_id=(row_peer(index // cols), col_peer(lax.rem(index, cols))),
            device_id_type=MESH,
        )
        return carry

    lax.fori_loop(1, rows * cols, greet, 0)

    def copy_to(src, dst, send, recv, row, col):
        return pltpu.make_async_remote_copy(
            src_ref=src, dst_ref=dst, send_sem=send, recv_sem=recv,
            device_id=(row, col), device_id_type=MESH,
        )

    def first_copy(z, x):
        return copy_to(
            first_out.at[x, z], first_in.at[side * cols + my_col],
            start_send.at[0], start_recv.at[0], hub_row, z * 2 + x,
        )

    def cores_copies(x, later):
        return [
            copy_to(
                cores.at[x, :, k * width:(k + 1) * width], hub_cores.at[my_x * 2 + side, k],
                start_send.at[1 + 2 * later], start_recv.at[1 + 2 * later],
                hub_row, my_z * 2 + x,
            )
            for k in (range(1, step_count - 1) if later else (0,))
        ]

    def lift_copy(d):
        return copy_to(
            lifts.at[my_row], lifts.at[my_row],
            start_send.at[2], start_recv.at[2], row_peer(d), my_col,
        )

    def older_copy(n, x):
        return copy_to(
            older_out.at[n - 1, x], older_in.at[n - 1, my_x * 2 + side],
            older_send.at[0], older_recv.at[n - 1], hub_row, my_z * 2 + x,
        )

    def drive_copy(n):
        return copy_to(
            drive.at[n, 0], drive.at[n, 0], drive_send.at[0], drive_recv.at[n], hub_row, my_col
        )

    def plane_copy(n, dy, dx):
        return copy_to(
            plane_proj.at[n, plane_pair], plane_proj.at[n, plane_pair],
            plane_send.at[0], plane_recv.at[n],
            2 * lax.rem(chip + dy, chips) + 1, my_z * 2 + lax.rem(my_x + dx, 2),
        )

    def pair_copy(n, d):
        return copy_to(
            pairs.at[n, own_pair], pairs.at[n, own_pair],
            pair_send.at[0], pair_recv.at[n], row_peer(d), my_col,
        )

    def sums_copy(n, z):
        return copy_to(
            sums_out.at[n - 1, z], sums_in.at[n - 1, my_z],
            sums_send.at[0], sums_recv.at[n - 1], my_row, z * 2 + my_x,
        )

    def last_copy(z, c):
        return copy_to(
            sums_out.at[step_count - 2, z, c], sums_in.at[step_count - 2, my_z, c],
            sums_send.at[1], sums_recv.at[step_count - 2], hub_row - 1 + c, z * 2 + my_x,
        )

    def tile_copy(n, part, owner, to):
        return copy_to(
            drive_tiles.at[n, part, owner], drive_tiles.at[n, part, owner],
            tile_send.at[0], tile_recv.at[n, part, owner // 2], to, my_col,
        )

    def pass_copy(n, part, owner):
        return copy_to(
            drive_tiles.at[n, part, owner], drive_tiles.at[n, part, owner],
            pass_send.at[0], pass_recv.at[n, part], partner, my_col,
        )

    def energy_copy(last, d):
        return copy_to(
            energy_own.at[step_count - 1] if last else energy_own.at[0:step_count - 1],
            energy_last.at[me] if last else energy_early.at[me],
            energy_send.at[last], energy_recv.at[last],
            row_peer(peers[d][0]), col_peer(peers[d][1]),
        )

    plane_peers = [(dy, dx) for dy in reversed(range(chips)) for dx in (1, 0) if dy or dx]

    def far_sum(n, x):
        depth = lag_count - n
        return jnp.dot(
            cores[x, :, n * width:],
            past_proj[0:depth].reshape(depth * width, fields),
            preferred_element_type=F32,
        ).astype(BF16)

    def near_base(n):
        depth = lag_count - n

        def add_slot(slot, carry):
            where = tiles_ref[0, 0, slot]
            value = jnp.dot(
                near_blocks[slot, :, n * tile:],
                history[where, 0:depth].reshape(depth * tile, fields),
                preferred_element_type=F32,
            )
            for lag in range(1, n):
                value += jnp.dot(
                    near_blocks[slot, :, lag * tile:(lag + 1) * tile],
                    fresh_tiles[n - 1 - lag][where],
                    preferred_element_type=F32,
                )
            near_sum[n] += value
            return carry

        near_sum[n] = jnp.zeros((tile, fields), F32)
        lax.fori_loop(0, slot_count, add_slot, 0)

    half = fields // 2

    def near_finish(n, parts):
        here = slice(parts[0] * half, (parts[-1] + 1) * half)
        total = near_sum[n, :, here]
        if n:
            for slot in range(slot_count):
                total += jnp.dot(
                    near_blocks[slot, :, 0:tile],
                    fresh_tiles[n - 1][tiles_ref[0, 0, slot], :, here],
                    preferred_element_type=F32,
                )
        driven = scaling[:, here] * (sources[n, :, here].astype(F32) - total)
        near_sum[n, :, here] = driven
        if n + 1 < step_count:
            sent = driven.astype(BF16)
            for part in parts:
                first = (part - parts[0]) * half
                drive_tiles[n, part, my_row] = sent[:, first:first + half]
                for d in range(2, rows, 2):
                    tile_copy(n, part, my_row, row_peer(d)).start()
                tile_copy(n, part, my_row, partner).start()
            drive[n, side, :, here] = jnp.dot(
                basis[my_row], sent, preferred_element_type=F32
            )
            if parts[-1] == 1:

                @pl.when(side == 0)
                def _():
                    drive_copy(n).start()

    def tiles_land(n, part):
        for d in range(2, rows, 2):
            tile_copy(n, part, row_peer(d), partner).wait_recv()
            pass_copy(n, part, row_peer(d)).start()

    def tiles_close(n, part):
        tile_copy(n, part, partner, partner).wait_recv()
        wait_bytes(drive_tiles.at[n, part, 0:chips - 1], pass_recv.at[n, part])

    def settle(n):
        far = lax.dot_general(
            target[...], pairs[n, my_row], (((0,), (0,)), ((), ())), preferred_element_type=F32
        )
        fresh = (near_sum[n] - scaling[...] * far).astype(BF16)
        steps_ref[n] = fresh
        if n + 1 < step_count:
            fresh_tiles[n][my_row] = fresh

    def rebuild(n, part):
        here = slice(part * half, (part + 1) * half)
        for d in range(1, rows):
            p = row_peer(d)
            far = lax.dot_general(
                lifts[p], pairs[n, p, :, here], (((0,), (0,)), ((), ())),
                preferred_element_type=F32,
            )
            fresh_tiles[n][p, :, here] = (drive_tiles[n, part, p].astype(F32) - far).astype(BF16)

    def measure_energy(n):
        energy_own[n] = (
            jnp.sum(jnp.square(steps_ref[n].astype(F32)), axis=0, keepdims=True) / panel_total
        )

    def publish(n, core):
        mine = core.astype(BF16)
        pairs[n, own_pair] = mine
        wait_bytes(drive.at[n, 0], drive_recv.at[n])
        mixed = jnp.dot(
            mixer[...], mine.reshape(2 * rank, fields), preferred_element_type=F32
        )
        plane_proj[n, plane_pair] = (
            drive[n] - mixed.reshape(2, rank, fields)
        ).astype(BF16)
        for dy, dx in plane_peers:
            plane_copy(n, dy, dx).start()
        for d in (rows - 1, *range(1, rows - 1)):
            pair_copy(n, d).start()

    lanes = stage.shape[2]
    block = stage.shape[1] // lag_count

    def spread(value, base=0):
        for c in range(value.shape[1] // lanes):
            stage[base + c, 0:value.shape[0]] = value[:, c * lanes:(c + 1) * lanes]

    def pick(lag, c, length):
        return stage[c, pl.ds(lag, length, stride=lag_count), :].astype(BF16)

    def pack_cores(z):
        span = 2 * rank
        here = pl.ds(z * span, span)
        base = z % (stage.shape[0] * lanes // width) * (width // lanes)
        total = None
        for p in range(rows):
            value = cores_raw[here, p].astype(F32).reshape(span * lag_count, rank).astype(BF16)
            place = (
                lax.broadcasted_iota(jnp.int32, (rank, width), 1)
                == lax.broadcasted_iota(jnp.int32, (rank, width), 0) + p * rank
            )
            term = jnp.dot(
                value, place.astype(F32).astype(BF16), preferred_element_type=F32
            )
            total = term if total is None else total + term
        spread(total, base)
        for lag in range(lag_count):
            for c in range(width // lanes):
                first = lag * width + c * lanes
                both = pick(lag, base + c, span)
                for x in range(2):
                    cores[x, z * rank:(z + 1) * rank, first:first + lanes] = (
                        both[x * rank:(x + 1) * rank]
                    )

    def pack_near(index, carry):
        slot = index // (tile // block)
        here = pl.ds(pl.multiple_of(lax.rem(index, tile // block) * block, block), block)
        spread(near_raw[slot, here].astype(F32).reshape(block * lag_count, tile))
        for lag in range(lag_count):
            for c in range(tile // lanes):
                first = lag * tile + c * lanes
                near_blocks[slot, here, first:first + lanes] = jnp.where(
                    slot < count_ref[0, 0], pick(lag, c, block), jnp.zeros((block, lanes), BF16)
                )
        return carry

    with scope("w_cores"):
        loads[1].wait()
        for load in (loads[2], *loads[5:]):
            load.start()
    with scope("pack_cores"):
        for z in range(depths):
            pack_cores(z)
        loads[0].wait()
    with scope("project"):
        for index, (first, length) in enumerate(spans):
            history_load(index).wait()
            for lag in range(first, first + length):
                for p in range(rows):
                    past_proj[lag, p] = jnp.dot(
                        basis[p], history[p, lag], preferred_element_type=F32
                    ).astype(BF16)

    for x in range(2):
        first_out[x] = far_sum(0, x).reshape(depths, rank, fields)
    with scope("barrier"):
        pl.semaphore_wait(barrier, rows * cols - 1)
    for i in range(depths - 1):
        for x in (1 - my_x, my_x):
            first_copy(far_depth(i), x).start()
    first_copy(my_z, 1 - my_x).start()

    @pl.when(is_hub)
    def _():
        first_in[cols + my_col] = first_out[my_x, my_z]

    @pl.when(side == 0)
    def _():
        first_copy(my_z, my_x).start()

    with scope("lifts"):
        for load in loads[3:5]:
            load.wait()
        lifts[my_row] = (target[...].astype(F32) * scaling_row[...]).astype(BF16)
        for d in range(1, rows):
            lift_copy(d).start()

    def send_older(n):
        for x in range(2):
            older_out[n - 1, x] = far_sum(n, x)
        older_copy(n, 1 - my_x).start()

        @pl.when(side == 0)
        def _():
            older_copy(n, my_x).start()

        @pl.when(is_hub)
        def _():
            older_in[n - 1, my_x * 2 + 1] = older_out[n - 1, my_x]

    def send_cores(later):
        for copy in cores_copies(1 - my_x, later):
            copy.start()

        @pl.when(side == 0)
        def _():
            for copy in cores_copies(my_x, later):
                copy.start()

        @pl.when(is_hub)
        def _():
            for k in range(1, step_count - 1) if later else (0,):
                hub_cores[my_x * 2 + 1, k] = cores[my_x, :, k * width:(k + 1) * width]

    with scope("older1"):
        send_cores(0)
        send_older(1)
    with scope("near0"):
        for load in (loads[2], *loads[6:]):
            load.wait()
        lax.fori_loop(0, slot_count * (tile // block), pack_near, 0)
        near_base(0)
        loads[5].wait()
        scaling[...] = jnp.transpose(jnp.broadcast_to(scaling_row[...], (fields, tile)))
        near_finish(0, (0, 1))
    with scope("w_lifts"):
        wait_bytes(lifts.at[0:rows - 1], start_recv.at[2])

    @pl.when(is_hub)
    def _():
        for c in range(2):
            own = lax.dot_general(
                basis[2 * chip + c], lifts[2 * chip + c], (((1,), (1,)), ((), ())),
                preferred_element_type=F32,
            ).astype(BF16)
            none = jnp.zeros((rank, rank), BF16)
            mixer[c * rank:(c + 1) * rank] = jnp.concatenate(
                [own, none] if c == 0 else [none, own], axis=1
            )
        with scope("w_first"):
            wait_bytes(first_in.at[0:2 * cols - 1], start_recv.at[0])
        core = []
        for c in range(2):
            total = first_in[c * cols].astype(F32)
            for j in range(1, cols):
                total += first_in[c * cols + j].astype(F32)
            core.append(total)
        publish(0, jnp.stack(core))

    with scope("older2"):
        send_cores(1)
        for n in range(2, step_count):
            send_older(n)

    def lead_rows(later):
        for k in range(1, step_count - 1) if later else (0,):
            for z in range(depths):
                for c in range(2):
                    for x in range(2):
                        lead[k, z * 2 + c, :, x * width:(x + 1) * width] = hub_cores[
                            x * 2 + c, k, z * rank:(z + 1) * rank
                        ]

    last = step_count - 1
    for n in range(1, step_count):
        with scope("near_base"):
            near_base(n)

        @pl.when(is_hub)
        def _():
            with scope("base"):
                if n == 1:
                    wait_bytes(hub_cores.at[0:3, 0], start_recv.at[1])
                    lead_rows(0)
                if n == 2:
                    wait_bytes(hub_cores.at[0:3, 1:], start_recv.at[3])
                    lead_rows(1)
                wait_bytes(older_in.at[n - 1, 0:3], older_recv.at[n - 1])
                for z in range(depths):
                    for c in range(2):
                        here = slice(z * rank, (z + 1) * rank)
                        sums_base[z * 2 + c] = older_in[n - 1, c, here].astype(
                            F32
                        ) + older_in[n - 1, 2 + c, here].astype(F32)
                for lag in range(1, n):
                    sums_base[...] += jnp.dot(
                        lead[lag].reshape(cols * rank, 2 * width),
                        plane_proj[n - 1 - lag].reshape(2 * width, fields),
                        preferred_element_type=F32,
                    ).reshape(cols, rank, fields)
            settle(n - 1)

        with scope("w_land0"):
            tiles_land(n - 1, 0)

        @pl.when(is_hub)
        def _():
            with scope("w_plane"):
                wait_bytes(plane_proj.at[n - 1, 0:2 * len(plane_peers)], plane_recv.at[n - 1])
            value = sums_base[...] + jnp.dot(
                lead[0].reshape(cols * rank, 2 * width),
                plane_proj[n - 1].reshape(2 * width, fields),
                preferred_element_type=F32,
            ).reshape(cols, rank, fields)
            sums_out[n - 1] = value.astype(BF16).reshape(depths, 2, rank, fields)
            for i in range(depths - 1):
                if n < last:
                    sums_copy(n, far_depth(i)).start()
                else:
                    last_copy(far_depth(i), 0).start()
                    last_copy(far_depth(i), 1).start()
            if n == last:
                last_copy(my_z, 0).start()
            sums_in[n - 1, my_z] = sums_out[n - 1, my_z]
            wait_bytes(pairs.at[n - 1, 0:2 * (chips - 1)], pair_recv.at[n - 1])

        with scope("w_tiles0"):
            tiles_close(n - 1, 0)

        @pl.when(side == 0)
        def _():
            with scope("w_pairs"):
                wait_bytes(pairs.at[n - 1], pair_recv.at[n - 1])
            settle(n - 1)

        with scope("w_tiles1"):
            tiles_land(n - 1, 1)
        with scope("finish0"):
            rebuild(n - 1, 0)
            if n + 1 < step_count:
                near_finish(n, (0,))
        with scope("w_tiles2"):
            tiles_close(n - 1, 1)
        with scope("finish1"):
            rebuild(n - 1, 1)
            near_finish(n, (1,) if n + 1 < step_count else (0, 1))
        measure_energy(n - 1)
        if n + 1 == step_count:
            for d in range(len(peers)):
                energy_copy(0, d).start()

        if n < last:

            @pl.when(is_hub)
            def _():
                with scope("w_sums"):
                    wait_bytes(sums_in.at[n - 1, 0:depths - 1], sums_recv.at[n - 1])
                total = sums_in[n - 1, 0].astype(F32)
                for z in range(1, depths):
                    total += sums_in[n - 1, z].astype(F32)
                publish(n, total)

    @pl.when(side == 0)
    def _():
        with scope("w_last"):
            wait_bytes(first_in.at[0:depths], sums_recv.at[last - 1])

    @pl.when(is_hub)
    def _():
        with scope("w_last"):
            wait_bytes(first_in.at[0:depths - 1], sums_recv.at[last - 1])

    total = sums_in[last - 1, 0, side].astype(F32)
    for z in range(1, depths):
        total += sums_in[last - 1, z, side].astype(F32)
    pairs[last, my_row] = total.astype(BF16)
    settle(last)
    measure_energy(last)
    for d in range(len(peers)):
        energy_copy(1, d).start()
    energy_early[me] = energy_own[0:last]
    energy_last[me] = energy_own[last]
    for group, where in ((0, energy_early), (1, energy_last)):
        with scope("w_energy"):
            wait_bytes(where.at[0:len(peers)], energy_recv.at[group])
        total = where[0]
        for origin in range(1, rows * cols):
            total += where[origin]
        if group:
            energy_ref[last:last + 1, :] = total
        else:
            for n in range(last):
                energy_ref[n:n + 1, :] = total[n]

    with scope("w_sends"):
        wait_bytes(lifts.at[0:rows - 1], start_send.at[2])
        wait_bytes(drive_tiles.at[:, :, 0:chips], tile_send.at[0])
        wait_bytes(drive_tiles.at[:, :, 0:chips - 1], pass_send.at[0])
        wait_bytes(energy_early.at[0:len(peers)], energy_send.at[0])
        wait_bytes(energy_last.at[0:len(peers)], energy_send.at[1])

        @pl.when(side == 0)
        def _():
            wait_bytes(first_in.at[0:cols], start_send.at[0])
            wait_bytes(hub_cores.at[0:2, 0], start_send.at[1])
            wait_bytes(hub_cores.at[0:2, 1:], start_send.at[3])
            wait_bytes(older_in.at[:, 0:2], older_send.at[0])
            wait_bytes(drive.at[:, 0], drive_send.at[0])

        @pl.when(is_hub)
        def _():
            wait_bytes(first_in.at[0:cols - 1], start_send.at[0])
            wait_bytes(hub_cores.at[0:1, 0], start_send.at[1])
            wait_bytes(hub_cores.at[0:1, 1:], start_send.at[3])
            wait_bytes(older_in.at[:, 0:1], older_send.at[0])
            wait_bytes(plane_proj.at[:, 0:2 * len(plane_peers)], plane_send.at[0])
            wait_bytes(plane_proj.at[:, 0:2 * (rows - 1)], pair_send.at[0])
            wait_bytes(sums_in.at[0:last - 1, 0:depths - 1], sums_send.at[0])
            wait_bytes(first_in.at[0:2 * depths - 1], sums_send.at[1])


def hand_over(steps_in, energy_in, steps_out, energy_out, sems):
    copies = (
        pltpu.make_async_copy(steps_in, steps_out, sems.at[0]),
        pltpu.make_async_copy(energy_in, energy_out, sems.at[1]),
    )
    for copy in copies:
        copy.start()
    for copy in copies:
        copy.wait()


def local(
    sources,
    history,
    inverse_diagonal,
    far_cores,
    target_basis,
    source_basis,
    near_blocks,
    near_tile,
    near_count,
):
    rows, _, lags, tile, fields = history.shape
    cols, rank = far_cores.shape[1:3]
    steps = sources.shape[2]
    slots = near_blocks.shape[2]
    panel_total = rows * cols * tile
    width = rows * rank
    depths = cols // 2
    lanes = min(128, tile, width)
    block = min(64, tile)
    dma = pltpu.SemaphoreType.DMA
    anywhere = pl.BlockSpec(memory_space=pltpu.HBM)
    inside = pl.BlockSpec(memory_space=pltpu.VMEM)
    new_steps, energies = pl.pallas_call(
        functools.partial(march, rows, cols, panel_total),
        out_shape=(
            pltpu.VMEM((steps, tile, fields), BF16),
            pltpu.VMEM((steps, fields), F32),
        ),
        in_specs=[anywhere] * 9,
        out_specs=(inside, inside),
        scratch_shapes=[
            pltpu.SMEM((1, 1, slots), jnp.int32),
            pltpu.SMEM((1, 1), jnp.int32),
            pltpu.VMEM((rows, rank, tile), BF16),
            pltpu.VMEM((rows, lags, tile, fields), BF16),
            pltpu.VMEM((2, depths * rank, lags * width), BF16),
            pltpu.VMEM((slots, tile, lags * tile), BF16),
            pltpu.VMEM((rank, tile), BF16),
            pltpu.VMEM((1, tile), F32),
            pltpu.VMEM((steps, tile, fields), BF16),
            pltpu.VMEM((tile, fields), F32),
            pltpu.VMEM((cols * rank, rows, lags, rank), BF16),
            pltpu.VMEM((slots, tile, lags, tile), BF16),
            pltpu.VMEM((max(tile, width) // lanes, block * lags, lanes), F32),
            pltpu.VMEM((lags, rows, rank, fields), BF16),
            pltpu.VMEM((rows, rank, tile), BF16),
            pltpu.VMEM((2 * rank, 2 * rank), BF16),
            pltpu.VMEM((4, steps - 1, depths * rank, width), BF16),
            pltpu.VMEM((steps - 1, cols, rank, 2 * width), BF16),
            pltpu.VMEM((steps - 1, 2, depths * rank, fields), BF16),
            pltpu.VMEM((steps - 1, 4, depths * rank, fields), BF16),
            pltpu.VMEM((2, depths, rank, fields), BF16),
            pltpu.VMEM((2 * cols, rank, fields), BF16),
            pltpu.VMEM((steps - 1, depths, 2, rank, fields), BF16),
            pltpu.VMEM((steps - 1, depths, 2, rank, fields), BF16),
            pltpu.VMEM((cols, rank, fields), F32),
            pltpu.VMEM((steps, rows, rank, fields), BF16),
            pltpu.VMEM((steps - 1, 2, rank, fields), F32),
            pltpu.VMEM((steps - 1, 2 * rows, rank, fields), BF16),
            pltpu.VMEM((steps - 1, 2, rows, tile, fields // 2), BF16),
            tuple(pltpu.VMEM((rows, tile, fields), BF16) for _ in range(steps - 1)),
            pltpu.VMEM((steps, tile, fields), F32),
            pltpu.VMEM((steps, 1, fields), F32),
            pltpu.VMEM((rows * cols, steps - 1, 1, fields), F32),
            pltpu.VMEM((rows * cols, 1, fields), F32),
            dma((8,)),
            dma(((lags + 1) // 2,)),
            dma((4,)),
            dma((4,)),
            dma((1,)),
            dma((steps - 1,)),
            dma((1,)),
            dma((steps - 1,)),
            dma((1,)),
            dma((steps - 1,)),
            dma((1,)),
            dma((steps - 1,)),
            dma((2,)),
            dma((steps - 1,)),
            dma((1,)),
            dma((steps - 1, 2, rows // 2)),
            dma((1,)),
            dma((steps - 1, 2)),
            dma((2,)),
            dma((2,)),
        ],
        compiler_params=pltpu.CompilerParams(
            collective_id=0, has_side_effects=True, vmem_limit_bytes=63 * 1024 * 1024
        ),
    )(
        near_tile,
        near_count,
        jnp.swapaxes(source_basis[:, 0], 1, 2),
        history[:, 0],
        far_cores.reshape(cols * rank, rows, lags, rank),
        near_blocks[0, 0],
        jnp.swapaxes(target_basis[0, 0], 0, 1),
        inverse_diagonal[0],
        sources[0, 0],
    )
    new_steps, energies = pl.pallas_call(
        hand_over,
        out_shape=(
            jax.ShapeDtypeStruct((steps, tile, fields), BF16),
            jax.ShapeDtypeStruct((steps, fields), F32),
        ),
        in_specs=(inside, inside),
        out_specs=(anywhere, anywhere),
        scratch_shapes=[dma((2,))],
    )(
        pltpu.with_memory_space_constraint(new_steps, pltpu.VMEM),
        pltpu.with_memory_space_constraint(energies, pltpu.VMEM),
    )
    return new_steps[None, None], energies


def solution(mesh):
    placed = (
        P("row", "col", None, None, None),
        P(None, "col", None, None, None),
        P("row", "col", None),
        P("row", None, None, None, "col", None, None),
        P("row", "col", None, None),
        P(None, "col", None, None),
        P("row", "col", None, None, None, None),
        P("row", "col", None),
        P("row", "col"),
    )
    return jax.shard_map(
        local,
        mesh=mesh,
        in_specs=placed,
        out_specs=(P("row", "col", None, None, None), P()),
        check_vma=False,
    )
```

time: 47.9 us -> 40.2 us (0.84)
  Pallas kernels: 46.5 us -> 38.8 us
    pallas_call x1, Pallas kernels: 45.7 us -> 37.9 us  [local(): pl.pallas_call(functools.partial(march, rows, cols, panel_total), out_sha...]
where the time goes in v2:
time: 40.2 us; the launch traced here: 40 us
  Pallas kernels  38.8 us (97%)
  between operations  1.29 us (3%)
    pallas_call x1, Pallas kernels, local(): pl.pallas_call(functools.partial(march, rows, cols, panel_total), out_sha...  37.9 us
    pallas_call x1, Pallas kernels, local(): pl.pallas_call(hand_over, out_shape=(jax.ShapeDtypeStruct((steps, tile, f...  0.81 us

profile of v2, /device:TPU:0, one launch (start us, length us, event | category | flops | bytes accessed | tf_op | source)
XLA Modules:
  0.0 40.0 jit_solution(8564294831662100949)
XLA Ops:
  1.3 37.9 %shard_map.104 = (bf16[4,256,256]{2,1,0:T(8,128)(2,1)S(1)}, f32[4,256]{1,0:T(4,128)S(1)}) custom-call(s32[1,1,3]{2,1,0:T(1,128)} %tiles_hbm.1, s32[1,1]{1,0:T(1,128)S(6)} %copy.11.count_hbm, bf16[4,32,256]{2,1,0:T(8,128)(2,1)} %bitcast.16, bf16[4,8,256,256]{3,2,1,0:T(8,128)(2,1)} %bitcast.12, bf16[256,4,8,32]{3,2,1,0:T(8,128)(2,1)} %bitcast.14, ...), custom_call_target="tpu_custom_call" | custom-call | tf_op jit(solution)/shard_map/pallas_call | solution.py:706
  39.2 0.8 %shard_map.105 = (bf16[4,256,256]{2,1,0:T(8,128)(2,1)}, f32[4,256]{1,0:T(4,128)}) custom-call(bf16[4,256,256]{2,1,0:T(8,128)(2,1)S(1)} %get-tuple-element.6.steps_in, f32[4,256]{1,0:T(4,128)S(1)} %get-tuple-element.7.energy_in), custom_call_target="tpu_custom_call" | custom-call | tf_op jit(solution)/shard_map/pallas_call | solution.py:784

commit v3 on v2

--- a/solution.py
+++ b/solution.py
@@ -44,6 +44,7 @@
     stage,
     past_proj,
     lifts,
+    weave,
     mixer,
     hub_cores,
     lead,
@@ -58,6 +59,8 @@
     drive,
     plane_proj,
     drive_tiles,
+    tile_pool,
+    core_pool,
     fresh_tiles,
     near_sum,
     energy_own,
@@ -65,23 +68,16 @@
     energy_last,
     load_sems,
     history_sems,
-    start_send,
+    send_sems,
     start_recv,
-    older_send,
+    cores_recv,
     older_recv,
-    drive_send,
     drive_recv,
-    plane_send,
     plane_recv,
-    pair_send,
     pair_recv,
-    sums_send,
     sums_recv,
-    tile_send,
     tile_recv,
-    pass_send,
     pass_recv,
-    energy_send,
     energy_recv,
 ):
     step_count = sources.shape[0]
@@ -171,78 +167,76 @@
     def first_copy(z, x):
         return copy_to(
             first_out.at[x, z], first_in.at[side * cols + my_col],
-            start_send.at[0], start_recv.at[0], hub_row, z * 2 + x,
-        )
-
-    def cores_copies(x, later):
-        return [
-            copy_to(
-                cores.at[x, :, k * width:(k + 1) * width], hub_cores.at[my_x * 2 + side, k],
-                start_send.at[1 + 2 * later], start_recv.at[1 + 2 * later],
-                hub_row, my_z * 2 + x,
-            )
-            for k in (range(1, step_count - 1) if later else (0,))
-        ]
+            load_sems.at[0], start_recv.at[0], hub_row, z * 2 + x,
+        )
+
+    def cores_copy(k, x):
+        return copy_to(
+            cores.at[x, :, k * width:(k + 1) * width], hub_cores.at[my_x * 2 + side, k],
+            load_sems.at[3], cores_recv.at[k], hub_row, my_z * 2 + x,
+        )
 
     def lift_copy(d):
         return copy_to(
             lifts.at[my_row], lifts.at[my_row],
-            start_send.at[2], start_recv.at[2], row_peer(d), my_col,
+            load_sems.at[1], start_recv.at[1], row_peer(d), my_col,
         )
 
     def older_copy(n, x):
         return copy_to(
             older_out.at[n - 1, x], older_in.at[n - 1, my_x * 2 + side],
-            older_send.at[0], older_recv.at[n - 1], hub_row, my_z * 2 + x,
+            load_sems.at[4], older_recv.at[n - 1], hub_row, my_z * 2 + x,
         )
 
     def drive_copy(n):
         return copy_to(
-            drive.at[n, 0], drive.at[n, 0], drive_send.at[0], drive_recv.at[n], hub_row, my_col
+            drive.at[n, 0], drive.at[n, 0], load_sems.at[2], drive_recv.at[n], hub_row, my_col
         )
 
     def plane_copy(n, dy, dx):
         return copy_to(
             plane_proj.at[n, plane_pair], plane_proj.at[n, plane_pair],
-            plane_send.at[0], plane_recv.at[n],
+            load_sems.at[5], plane_recv.at[n],
             2 * lax.rem(chip + dy, chips) + 1, my_z * 2 + lax.rem(my_x + dx, 2),
         )
 
     def pair_copy(n, d):
         return copy_to(
             pairs.at[n, own_pair], pairs.at[n, own_pair],
-            pair_send.at[0], pair_recv.at[n], row_peer(d), my_col,
+            load_sems.at[6], pair_recv.at[n], row_peer(d), my_col,
         )
 
     def sums_copy(n, z):
         return copy_to(
             sums_out.at[n - 1, z], sums_in.at[n - 1, my_z],
-            sums_send.at[0], sums_recv.at[n - 1], my_row, z * 2 + my_x,
+            send_sems.at[2], sums_recv.at[n - 1], my_row, z * 2 + my_x,
         )
 
     def last_copy(z, c):
         return copy_to(
             sums_out.at[step_count - 2, z, c], sums_in.at[step_count - 2, my_z, c],
-            sums_send.at[1], sums_recv.at[step_count - 2], hub_row - 1 + c, z * 2 + my_x,
-        )
-
-    def tile_copy(n, part, owner, to):
+            load_sems.at[7], sums_recv.at[step_count - 2], hub_row - 1 + c, z * 2 + my_x,
+        )
+
+    def tile_copy(n, part, owner, to, index):
         return copy_to(
             drive_tiles.at[n, part, owner], drive_tiles.at[n, part, owner],
-            tile_send.at[0], tile_recv.at[n, part, owner // 2], to, my_col,
+            history_sems.at[0],
+            pass_recv.at[n, part] if index is None else tile_recv.at[n, part, index],
+            to, my_col,
         )
 
     def pass_copy(n, part, owner):
         return copy_to(
             drive_tiles.at[n, part, owner], drive_tiles.at[n, part, owner],
-            pass_send.at[0], pass_recv.at[n, part], partner, my_col,
+            history_sems.at[1], pass_recv.at[n, part], partner, my_col,
         )
 
     def energy_copy(last, d):
         return copy_to(
             energy_own.at[step_count - 1] if last else energy_own.at[0:step_count - 1],
             energy_last.at[me] if last else energy_early.at[me],
-            energy_send.at[last], energy_recv.at[last],
+            send_sems.at[last], energy_recv.at[last],
             row_peer(peers[d][0]), col_peer(peers[d][1]),
         )
 
@@ -280,30 +274,68 @@
 
     half = fields // 2
 
-    def near_finish(n, parts):
-        here = slice(parts[0] * half, (parts[-1] + 1) * half)
+    def send_tiles(n, part):
+        for d in range(2, rows, 2):
+            tile_copy(n, part, my_row, row_peer(d), (rows - d) // 2 - 1).start()
+
+    def near_tiles(n, part):
+        here = slice(part * half, (part + 1) * half)
+        tile_pool[...] = drive_tiles[n - 1, part]
         total = near_sum[n, :, here]
-        if n:
-            for slot in range(slot_count):
-                total += jnp.dot(
-                    near_blocks[slot, :, 0:tile],
-                    fresh_tiles[n - 1][tiles_ref[0, 0, slot], :, here],
-                    preferred_element_type=F32,
-                )
+        for slot in range(slot_count):
+            total += jnp.dot(
+                near_blocks[slot, :, 0:tile],
+                tile_pool[tiles_ref[0, 0, slot]],
+                preferred_element_type=F32,
+            )
+        near_sum[n, :, here] = total
+
+    def near_first():
+        driven = scaling[...] * (sources[0].astype(F32) - near_sum[0])
+        near_sum[0] = driven
+        sent = driven.astype(BF16)
+        drive[0, side] = jnp.dot(basis[my_row], sent, preferred_element_type=F32)
+
+        @pl.when(side == 0)
+        def _():
+            drive_copy(0).start()
+
+        for part in range(2):
+            drive_tiles[0, part, my_row] = sent[:, part * half:(part + 1) * half]
+        send_tiles(0, 0)
+
+        @pl.when(side == 0)
+        def _():
+            send_tiles(0, 1)
+
+        for part in range(2):
+            tile_copy(0, part, my_row, partner, None).start()
+
+    def near_finish(n, part):
+        here = slice(part * half, (part + 1) * half)
+        core_pool[...] = pairs[n - 1, :, :, here]
+        known = [core_pool[tiles_ref[0, 0, slot]] for slot in range(slot_count)]
+        total = near_sum[n, :, here] - jnp.dot(
+            weave[...], jnp.concatenate(known, axis=0), preferred_element_type=F32
+        )
         driven = scaling[:, here] * (sources[n, :, here].astype(F32) - total)
         near_sum[n, :, here] = driven
         if n + 1 < step_count:
             sent = driven.astype(BF16)
-            for part in parts:
-                first = (part - parts[0]) * half
-                drive_tiles[n, part, my_row] = sent[:, first:first + half]
-                for d in range(2, rows, 2):
-                    tile_copy(n, part, my_row, row_peer(d)).start()
-                tile_copy(n, part, my_row, partner).start()
+            drive_tiles[n, part, my_row] = sent
+            if part == 0:
+                send_tiles(n, part)
+            else:
+
+                @pl.when(side == 0)
+                def _():
+                    send_tiles(n, part)
+
+            tile_copy(n, part, my_row, partner, None).start()
             drive[n, side, :, here] = jnp.dot(
                 basis[my_row], sent, preferred_element_type=F32
             )
-            if parts[-1] == 1:
+            if part == 1:
 
                 @pl.when(side == 0)
                 def _():
@@ -311,36 +343,35 @@
 
     def tiles_land(n, part):
         for d in range(2, rows, 2):
-            tile_copy(n, part, row_peer(d), partner).wait_recv()
+            tile_copy(n, part, row_peer(d), partner, d // 2 - 1).wait_recv()
             pass_copy(n, part, row_peer(d)).start()
 
     def tiles_close(n, part):
-        tile_copy(n, part, partner, partner).wait_recv()
-        wait_bytes(drive_tiles.at[n, part, 0:chips - 1], pass_recv.at[n, part])
+        wait_bytes(drive_tiles.at[n, part, 0:chips], pass_recv.at[n, part])
 
     def settle(n):
         far = lax.dot_general(
             target[...], pairs[n, my_row], (((0,), (0,)), ((), ())), preferred_element_type=F32
         )
         fresh = (near_sum[n] - scaling[...] * far).astype(BF16)
+        energy_own[n] = (
+            jnp.sum(jnp.square(fresh.astype(F32)), axis=0, keepdims=True) / panel_total
+        )
         steps_ref[n] = fresh
         if n + 1 < step_count:
             fresh_tiles[n][my_row] = fresh
 
-    def rebuild(n, part):
-        here = slice(part * half, (part + 1) * half)
+    def rebuild(n):
         for d in range(1, rows):
             p = row_peer(d)
             far = lax.dot_general(
-                lifts[p], pairs[n, p, :, here], (((0,), (0,)), ((), ())),
-                preferred_element_type=F32,
+                lifts[p], pairs[n, p], (((0,), (0,)), ((), ())), preferred_element_type=F32
             )
-            fresh_tiles[n][p, :, here] = (drive_tiles[n, part, p].astype(F32) - far).astype(BF16)
-
-    def measure_energy(n):
-        energy_own[n] = (
-            jnp.sum(jnp.square(steps_ref[n].astype(F32)), axis=0, keepdims=True) / panel_total
-        )
+            for part in range(2):
+                here = slice(part * half, (part + 1) * half)
+                fresh_tiles[n][p, :, here] = (
+                    drive_tiles[n, part, p].astype(F32) - far[:, here]
+                ).astype(BF16)
 
     def publish(n, core):
         mine = core.astype(BF16)
@@ -354,7 +385,10 @@
         ).astype(BF16)
         for dy, dx in plane_peers:
             plane_copy(n, dy, dx).start()
-        for d in (rows - 1, *range(1, rows - 1)):
+        for d in (rows - 1, *range(1, rows - 1, 2)):
+            pair_copy(n, d).start()
+        send_tiles(n, 1)
+        for d in range(2, rows - 1, 2):
             pair_copy(n, d).start()
 
     lanes = stage.shape[2]
@@ -392,16 +426,22 @@
                         both[x * rank:(x + 1) * rank]
                     )
 
-    def pack_near(index, carry):
+    def pack_block(index, base):
         slot = index // (tile // block)
         here = pl.ds(pl.multiple_of(lax.rem(index, tile // block) * block, block), block)
-        spread(near_raw[slot, here].astype(F32).reshape(block * lag_count, tile))
+        spread(near_raw[slot, here].astype(F32).reshape(block * lag_count, tile), base)
         for lag in range(lag_count):
             for c in range(tile // lanes):
                 first = lag * tile + c * lanes
                 near_blocks[slot, here, first:first + lanes] = jnp.where(
-                    slot < count_ref[0, 0], pick(lag, c, block), jnp.zeros((block, lanes), BF16)
+                    slot < count_ref[0, 0], pick(lag, base + c, block), jnp.zeros((block, lanes), BF16)
                 )
+
+    turns = stage.shape[0] * lanes // tile
+
+    def pack_near(index, carry):
+        for turn in range(turns):
+            pack_block(index * turns + turn, turn * (tile // lanes))
         return carry
 
     with scope("w_cores"):
@@ -438,12 +478,11 @@
     def _():
         first_copy(my_z, my_x).start()
 
-    with scope("lifts"):
-        for load in loads[3:5]:
-            load.wait()
-        lifts[my_row] = (target[...].astype(F32) * scaling_row[...]).astype(BF16)
-        for d in range(1, rows):
-            lift_copy(d).start()
+    for load in loads[3:5]:
+        load.wait()
+    lifts[my_row] = (target[...].astype(F32) * scaling_row[...]).astype(BF16)
+    for d in range(1, rows):
+        lift_copy(d).start()
 
     def send_older(n):
         for x in range(2):
@@ -458,33 +497,42 @@
         def _():
             older_in[n - 1, my_x * 2 + 1] = older_out[n - 1, my_x]
 
-    def send_cores(later):
-        for copy in cores_copies(1 - my_x, later):
-            copy.start()
+    def send_cores(k):
+        cores_copy(k, 1 - my_x).start()
 
         @pl.when(side == 0)
         def _():
-            for copy in cores_copies(my_x, later):
-                copy.start()
+            cores_copy(k, my_x).start()
 
         @pl.when(is_hub)
         def _():
-            for k in range(1, step_count - 1) if later else (0,):
-                hub_cores[my_x * 2 + 1, k] = cores[my_x, :, k * width:(k + 1) * width]
+            hub_cores[my_x * 2 + 1, k] = cores[my_x, :, k * width:(k + 1) * width]
 
     with scope("older1"):
         send_cores(0)
         send_older(1)
-    with scope("near0"):
+    with scope("pack_near"):
         for load in (loads[2], *loads[6:]):
             load.wait()
-        lax.fori_loop(0, slot_count * (tile // block), pack_near, 0)
+        lax.fori_loop(0, slot_count * (tile // block) // turns, pack_near, 0)
+    with scope("near_base0"):
         near_base(0)
+    with scope("near0"):
         loads[5].wait()
         scaling[...] = jnp.transpose(jnp.broadcast_to(scaling_row[...], (fields, tile)))
-        near_finish(0, (0, 1))
+        near_first()
     with scope("w_lifts"):
-        wait_bytes(lifts.at[0:rows - 1], start_recv.at[2])
+        wait_bytes(lifts.at[0:rows - 1], start_recv.at[1])
+    weave[...] = jnp.concatenate(
+        [
+            lax.dot_general(
+                near_blocks[slot, :, 0:tile], lifts[tiles_ref[0, 0, slot]],
+                (((1,), (1,)), ((), ())), preferred_element_type=F32,
+            )
+            for slot in range(slot_count)
+        ],
+        axis=1,
+    ).astype(BF16)
 
     @pl.when(is_hub)
     def _():
@@ -507,34 +555,28 @@
             core.append(total)
         publish(0, jnp.stack(core))
 
-    with scope("older2"):
-        send_cores(1)
-        for n in range(2, step_count):
-            send_older(n)
-
-    def lead_rows(later):
-        for k in range(1, step_count - 1) if later else (0,):
-            for z in range(depths):
-                for c in range(2):
-                    for x in range(2):
-                        lead[k, z * 2 + c, :, x * width:(x + 1) * width] = hub_cores[
-                            x * 2 + c, k, z * rank:(z + 1) * rank
-                        ]
+    def lead_rows(k):
+        for z in range(depths):
+            for c in range(2):
+                for x in range(2):
+                    lead[k, z * 2 + c, :, x * width:(x + 1) * width] = hub_cores[
+                        x * 2 + c, k, z * rank:(z + 1) * rank
+                    ]
 
     last = step_count - 1
     for n in range(1, step_count):
+        if n > 1:
+            with scope("settle"):
+                settle(n - 2)
+                rebuild(n - 2)
         with scope("near_base"):
             near_base(n)
 
         @pl.when(is_hub)
         def _():
             with scope("base"):
-                if n == 1:
-                    wait_bytes(hub_cores.at[0:3, 0], start_recv.at[1])
-                    lead_rows(0)
-                if n == 2:
-                    wait_bytes(hub_cores.at[0:3, 1:], start_recv.at[3])
-                    lead_rows(1)
+                wait_bytes(hub_cores.at[0:3, n - 1], cores_recv.at[n - 1])
+                lead_rows(n - 1)
                 wait_bytes(older_in.at[n - 1, 0:3], older_recv.at[n - 1])
                 for z in range(depths):
                     for c in range(2):
@@ -548,7 +590,6 @@
                         plane_proj[n - 1 - lag].reshape(2 * width, fields),
                         preferred_element_type=F32,
                     ).reshape(cols, rank, fields)
-            settle(n - 1)
 
         with scope("w_land0"):
             tiles_land(n - 1, 0)
@@ -572,30 +613,37 @@
             if n == last:
                 last_copy(my_z, 0).start()
             sums_in[n - 1, my_z] = sums_out[n - 1, my_z]
-            wait_bytes(pairs.at[n - 1, 0:2 * (chips - 1)], pair_recv.at[n - 1])
 
         with scope("w_tiles0"):
             tiles_close(n - 1, 0)
+        with scope("tiles0"):
+            near_tiles(n, 0)
+        with scope("w_tiles1"):
+            tiles_land(n - 1, 1)
+        if n < last:
+            with scope("older"):
+                send_cores(n)
+                send_older(n + 1)
+
+        @pl.when(is_hub)
+        def _():
+            with scope("w_pairs"):
+                wait_bytes(pairs.at[n - 1, 0:2 * (chips - 1)], pair_recv.at[n - 1])
 
         @pl.when(side == 0)
         def _():
             with scope("w_pairs"):
                 wait_bytes(pairs.at[n - 1], pair_recv.at[n - 1])
-            settle(n - 1)
-
-        with scope("w_tiles1"):
-            tiles_land(n - 1, 1)
+
         with scope("finish0"):
-            rebuild(n - 1, 0)
-            if n + 1 < step_count:
-                near_finish(n, (0,))
+            near_finish(n, 0)
         with scope("w_tiles2"):
             tiles_close(n - 1, 1)
         with scope("finish1"):
-            rebuild(n - 1, 1)
-            near_finish(n, (1,) if n + 1 < step_count else (0, 1))
-        measure_energy(n - 1)
-        if n + 1 == step_count:
+            near_tiles(n, 1)
+            near_finish(n, 1)
+        if n == last:
+            settle(n - 1)
             for d in range(len(peers)):
                 energy_copy(0, d).start()
 
@@ -625,7 +673,6 @@
         total += sums_in[last - 1, z, side].astype(F32)
     pairs[last, my_row] = total.astype(BF16)
     settle(last)
-    measure_energy(last)
     for d in range(len(peers)):
         energy_copy(1, d).start()
     energy_early[me] = energy_own[0:last]
@@ -643,30 +690,28 @@
                 energy_ref[n:n + 1, :] = total[n]
 
     with scope("w_sends"):
-        wait_bytes(lifts.at[0:rows - 1], start_send.at[2])
-        wait_bytes(drive_tiles.at[:, :, 0:chips], tile_send.at[0])
-        wait_bytes(drive_tiles.at[:, :, 0:chips - 1], pass_send.at[0])
-        wait_bytes(energy_early.at[0:len(peers)], energy_send.at[0])
-        wait_bytes(energy_last.at[0:len(peers)], energy_send.at[1])
+        wait_bytes(lifts.at[0:rows - 1], load_sems.at[1])
+        wait_bytes(drive_tiles.at[:, :, 0:chips], history_sems.at[0])
+        wait_bytes(drive_tiles.at[:, :, 0:chips - 1], history_sems.at[1])
+        wait_bytes(energy_early.at[0:len(peers)], send_sems.at[0])
+        wait_bytes(energy_last.at[0:len(peers)], send_sems.at[1])
 
         @pl.when(side == 0)
         def _():
-            wait_bytes(first_in.at[0:cols], start_send.at[0])
-            wait_bytes(hub_cores.at[0:2, 0], start_send.at[1])
-            wait_bytes(hub_cores.at[0:2, 1:], start_send.at[3])
-            wait_bytes(older_in.at[:, 0:2], older_send.at[0])
-            wait_bytes(drive.at[:, 0], drive_send.at[0])
+            wait_bytes(first_in.at[0:cols], load_sems.at[0])
+            wait_bytes(hub_cores.at[0:2], load_sems.at[3])
+            wait_bytes(older_in.at[:, 0:2], load_sems.at[4])
+            wait_bytes(drive.at[:, 0], load_sems.at[2])
 
         @pl.when(is_hub)
         def _():
-            wait_bytes(first_in.at[0:cols - 1], start_send.at[0])
-            wait_bytes(hub_cores.at[0:1, 0], start_send.at[1])
-            wait_bytes(hub_cores.at[0:1, 1:], start_send.at[3])
-            wait_bytes(older_in.at[:, 0:1], older_send.at[0])
-            wait_bytes(plane_proj.at[:, 0:2 * len(plane_peers)], plane_send.at[0])
-            wait_bytes(plane_proj.at[:, 0:2 * (rows - 1)], pair_send.at[0])
-            wait_bytes(sums_in.at[0:last - 1, 0:depths - 1], sums_send.at[0])
-            wait_bytes(first_in.at[0:2 * depths - 1], sums_send.at[1])
+            wait_bytes(first_in.at[0:cols - 1], load_sems.at[0])
+            wait_bytes(hub_cores.at[0:1], load_sems.at[3])
+            wait_bytes(older_in.at[:, 0:1], load_sems.at[4])
+            wait_bytes(plane_proj.at[:, 0:2 * len(plane_peers)], load_sems.at[5])
+            wait_bytes(plane_proj.at[:, 0:2 * (rows - 1)], load_sems.at[6])
+            wait_bytes(sums_in.at[0:last - 1, 0:depths - 1], send_sems.at[2])
+            wait_bytes(first_in.at[0:2 * depths - 1], load_sems.at[7])
 
 
 def hand_over(steps_in, energy_in, steps_out, energy_out, sems):
@@ -724,9 +769,10 @@
             pltpu.VMEM((tile, fields), F32),
             pltpu.VMEM((cols * rank, rows, lags, rank), BF16),
             pltpu.VMEM((slots, tile, lags, tile), BF16),
-            pltpu.VMEM((max(tile, width) // lanes, block * lags, lanes), F32),
+            pltpu.VMEM((max(2 * tile, width) // lanes, block * lags, lanes), F32),
             pltpu.VMEM((lags, rows, rank, fields), BF16),
             pltpu.VMEM((rows, rank, tile), BF16),
+            pltpu.VMEM((tile, slots * rank), BF16),
             pltpu.VMEM((2 * rank, 2 * rank), BF16),
             pltpu.VMEM((4, steps - 1, depths * rank, width), BF16),
             pltpu.VMEM((steps - 1, cols, rank, 2 * width), BF16),
@@ -741,6 +787,8 @@
             pltpu.VMEM((steps - 1, 2, rank, fields), F32),
             pltpu.VMEM((steps - 1, 2 * rows, rank, fields), BF16),
             pltpu.VMEM((steps - 1, 2, rows, tile, fields // 2), BF16),
+            pltpu.VMEM((rows, tile, fields // 2), BF16),
+            pltpu.VMEM((rows, rank, fields // 2), BF16),
             tuple(pltpu.VMEM((rows, tile, fields), BF16) for _ in range(steps - 1)),
             pltpu.VMEM((steps, tile, fields), F32),
             pltpu.VMEM((steps, 1, fields), F32),
@@ -748,23 +796,16 @@
             pltpu.VMEM((rows * cols, 1, fields), F32),
             dma((8,)),
             dma(((lags + 1) // 2,)),
-            dma((4,)),
-            dma((4,)),
-            dma((1,)),
-            dma((steps - 1,)),
-            dma((1,)),
-            dma((steps - 1,)),
-            dma((1,)),
-            dma((steps - 1,)),
-            dma((1,)),
-            dma((steps - 1,)),
+            dma((3,)),
             dma((2,)),
             dma((steps - 1,)),
-            dma((1,)),
-            dma((steps - 1, 2, rows // 2)),
-            dma((1,)),
+            dma((steps - 1,)),
+            dma((steps - 1,)),
+            dma((steps - 1,)),
+            dma((steps - 1,)),
+            dma((steps - 1,)),
+            dma((steps - 1, 2, rows // 2 - 1)),
             dma((steps - 1, 2)),
-            dma((2,)),
             dma((2,)),
         ],
         compiler_params=pltpu.CompilerParams(

time: 40.2 us -> 38.8 us (0.965)
  Pallas kernels: 38.8 us -> 37.4 us
    pallas_call x1, Pallas kernels: 37.9 us -> 36.6 us  [local(): pl.pallas_call(functools.partial(march, rows, cols, panel_total), out_sha...]
where the time goes in v3:
time: 38.8 us; the launch traced here: 38.7 us
  Pallas kernels  37.4 us (96%)
  between operations  1.29 us (3%)
    pallas_call x1, Pallas kernels, local(): pl.pallas_call(functools.partial(march, rows, cols, panel_total), out_sha...  36.6 us
    pallas_call x1, Pallas kernels, local(): pl.pallas_call(hand_over, out_shape=(jax.ShapeDtypeStruct((steps, tile, f...  0.81 us

profile of v3, /device:TPU:0, one launch (start us, length us, event | category | flops | bytes accessed | tf_op | source)
XLA Modules:
  0.0 38.7 jit_solution(7666940264265975501)
XLA Ops:
  1.3 36.6 %shard_map.104 = (bf16[4,256,256]{2,1,0:T(8,128)(2,1)S(1)}, f32[4,256]{1,0:T(4,128)S(1)}) custom-call(s32[1,1,3]{2,1,0:T(1,128)} %tiles_hbm.1, s32[1,1]{1,0:T(1,128)S(6)} %copy.11.count_hbm, bf16[4,32,256]{2,1,0:T(8,128)(2,1)} %bitcast.16, bf16[4,8,256,256]{3,2,1,0:T(8,128)(2,1)} %bitcast.12, bf16[256,4,8,32]{3,2,1,0:T(8,128)(2,1)} %bitcast.14, ...), custom_call_target="tpu_custom_call" | custom-call | tf_op jit(solution)/shard_map/pallas_call | solution.py:751
  37.8 0.8 %shard_map.105 = (bf16[4,256,256]{2,1,0:T(8,128)(2,1)}, f32[4,256]{1,0:T(4,128)}) custom-call(bf16[4,256,256]{2,1,0:T(8,128)(2,1)S(1)} %get-tuple-element.6.steps_in, f32[4,256]{1,0:T(4,128)S(1)} %get-tuple-element.7.energy_in), custom_call_target="tpu_custom_call" | custom-call | tf_op jit(solution)/shard_map/pallas_call | solution.py:825

commit v4 on v3

--- a/solution.py
+++ b/solution.py
@@ -209,7 +209,7 @@
     def sums_copy(n, z):
         return copy_to(
             sums_out.at[n - 1, z], sums_in.at[n - 1, my_z],
-            send_sems.at[2], sums_recv.at[n - 1], my_row, z * 2 + my_x,
+            send_sems.at[3], sums_recv.at[n - 1], my_row, z * 2 + my_x,
         )
 
     def last_copy(z, c):
@@ -234,8 +234,8 @@
 
     def energy_copy(last, d):
         return copy_to(
-            energy_own.at[step_count - 1] if last else energy_own.at[0:step_count - 1],
-            energy_last.at[me] if last else energy_early.at[me],
+            energy_own.at[step_count - 3 + last] if last else energy_own.at[0:step_count - 2],
+            energy_last.at[last - 1, me] if last else energy_early.at[me],
             send_sems.at[last], energy_recv.at[last],
             row_peer(peers[d][0]), col_peer(peers[d][1]),
         )
@@ -569,6 +569,9 @@
             with scope("settle"):
                 settle(n - 2)
                 rebuild(n - 2)
+            if n == last:
+                for d in range(len(peers)):
+                    energy_copy(0, d).start()
         with scope("near_base"):
             near_base(n)
 
@@ -645,7 +648,7 @@
         if n == last:
             settle(n - 1)
             for d in range(len(peers)):
-                energy_copy(0, d).start()
+                energy_copy(1, d).start()
 
         if n < last:
 
@@ -674,19 +677,19 @@
     pairs[last, my_row] = total.astype(BF16)
     settle(last)
     for d in range(len(peers)):
-        energy_copy(1, d).start()
-    energy_early[me] = energy_own[0:last]
-    energy_last[me] = energy_own[last]
-    for group, where in ((0, energy_early), (1, energy_last)):
-        with scope("w_energy"):
-            wait_bytes(where.at[0:len(peers)], energy_recv.at[group])
+        energy_copy(2, d).start()
+    energy_early[me] = energy_own[0:last - 1]
+    energy_last[0, me] = energy_own[last - 1]
+    energy_last[1, me] = energy_own[last]
+    for group, where in enumerate((energy_early, energy_last.at[0], energy_last.at[1])):
+        wait_bytes(where.at[0:len(peers)], energy_recv.at[group])
         total = where[0]
         for origin in range(1, rows * cols):
             total += where[origin]
         if group:
-            energy_ref[last:last + 1, :] = total
+            energy_ref[last - 2 + group:last - 1 + group, :] = total
         else:
-            for n in range(last):
+            for n in range(last - 1):
                 energy_ref[n:n + 1, :] = total[n]
 
     with scope("w_sends"):
@@ -694,7 +697,8 @@
         wait_bytes(drive_tiles.at[:, :, 0:chips], history_sems.at[0])
         wait_bytes(drive_tiles.at[:, :, 0:chips - 1], history_sems.at[1])
         wait_bytes(energy_early.at[0:len(peers)], send_sems.at[0])
-        wait_bytes(energy_last.at[0:len(peers)], send_sems.at[1])
+        wait_bytes(energy_last.at[0, 0:len(peers)], send_sems.at[1])
+        wait_bytes(energy_last.at[1, 0:len(peers)], send_sems.at[2])
 
         @pl.when(side == 0)
         def _():
@@ -710,7 +714,7 @@
             wait_bytes(older_in.at[:, 0:1], load_sems.at[4])
             wait_bytes(plane_proj.at[:, 0:2 * len(plane_peers)], load_sems.at[5])
             wait_bytes(plane_proj.at[:, 0:2 * (rows - 1)], load_sems.at[6])
-            wait_bytes(sums_in.at[0:last - 1, 0:depths - 1], send_sems.at[2])
+            wait_bytes(sums_in.at[0:last - 1, 0:depths - 1], send_sems.at[3])
             wait_bytes(first_in.at[0:2 * depths - 1], load_sems.at[7])
 
 
@@ -792,11 +796,11 @@
             tuple(pltpu.VMEM((rows, tile, fields), BF16) for _ in range(steps - 1)),
             pltpu.VMEM((steps, tile, fields), F32),
             pltpu.VMEM((steps, 1, fields), F32),
-            pltpu.VMEM((rows * cols, steps - 1, 1, fields), F32),
-            pltpu.VMEM((rows * cols, 1, fields), F32),
+            pltpu.VMEM((rows * cols, steps - 2, 1, fields), F32),
+            pltpu.VMEM((2, rows * cols, 1, fields), F32),
             dma((8,)),
             dma(((lags + 1) // 2,)),
-            dma((3,)),
+            dma((4,)),
             dma((2,)),
             dma((steps - 1,)),
             dma((steps - 1,)),
@@ -806,7 +810,7 @@
             dma((steps - 1,)),
             dma((steps - 1, 2, rows // 2 - 1)),
             dma((steps - 1, 2)),
-            dma((2,)),
+            dma((3,)),
         ],
         compiler_params=pltpu.CompilerParams(
             collective_id=0, has_side_effects=True, vmem_limit_bytes=63 * 1024 * 1024

time: 38.8 us -> 39.2 us (1.010)
  Pallas kernels: 37.4 us -> 37.8 us
    pallas_call x1, Pallas kernels: 36.6 us -> 37 us  [local(): pl.pallas_call(functools.partial(march, rows, cols, panel_total), out_sha...]
where the time goes in v4:
time: 39.2 us; the launch traced here: 39.1 us
  Pallas kernels  37.8 us (96%)
  between operations  1.29 us (3%)
    pallas_call x1, Pallas kernels, local(): pl.pallas_call(functools.partial(march, rows, cols, panel_total), out_sha...  37 us
    pallas_call x1, Pallas kernels, local(): pl.pallas_call(hand_over, out_shape=(jax.ShapeDtypeStruct((steps, tile, f...  0.81 us

profile of v4, /device:TPU:0, one launch (start us, length us, event | category | flops | bytes accessed | tf_op | source)
XLA Modules:
  0.0 39.1 jit_solution(10296222914184692543)
XLA Ops:
  1.3 37.0 %shard_map.104 = (bf16[4,256,256]{2,1,0:T(8,128)(2,1)S(1)}, f32[4,256]{1,0:T(4,128)S(1)}) custom-call(s32[1,1,3]{2,1,0:T(1,128)} %tiles_hbm.1, s32[1,1]{1,0:T(1,128)S(6)} %copy.11.count_hbm, bf16[4,32,256]{2,1,0:T(8,128)(2,1)} %bitcast.16, bf16[4,8,256,256]{3,2,1,0:T(8,128)(2,1)} %bitcast.12, bf16[256,4,8,32]{3,2,1,0:T(8,128)(2,1)} %bitcast.14, ...), custom_call_target="tpu_custom_call" | custom-call | tf_op jit(solution)/shard_map/pallas_call | solution.py:755
  38.3 0.8 %shard_map.105 = (bf16[4,256,256]{2,1,0:T(8,128)(2,1)}, f32[4,256]{1,0:T(4,128)}) custom-call(bf16[4,256,256]{2,1,0:T(8,128)(2,1)S(1)} %get-tuple-element.6.steps_in, f32[4,256]{1,0:T(4,128)S(1)} %get-tuple-element.7.energy_in), custom_call_target="tpu_custom_call" | custom-call | tf_op jit(solution)/shard_map/pallas_call | solution.py:829
